TPU v7x, 32 devices: a whole 2x2x4 slice. The times are simulated.
32 devices in a mesh: scen: 8 (over z, y), gen: 4 (over x, core).
Axes of the slice: x: 2, y: 2, z: 4, core: 2. Of those that a mesh axis runs over, the one named last changes fastest.
Arguments:
- zone_load: float32 [128, 16, 256], P('scen'), may hold values from 0.3 to 1
- linear_cost: float32 [16, 20480], P(None, 'gen'), may hold values from -4 to 4
- cost_diag: float32 [20480], P('gen'), may hold values from 0.5 to 2
- capacity: float32 [20480], P('gen'), may hold values from 0.5 to 2
- cost_tiles: bfloat16 [80, 256, 256], P('gen'), may hold values from -0.375 to 0.375
- coupling_tiles: bfloat16 [8, 80, 256, 256], P('scen', 'gen'), may hold values from -0.375 to 0.375
- block_map: int32 [8, 80], P('scen', 'gen'), may hold values 0 or 1
- zone_index: int32 [20480], P('gen'), may hold values from 0 to 255
- step_numer: int32 [5], replicated, may hold values from 1 to 4
- step_denom: int32 [5], replicated, may hold values from 5 to 8
Outputs:
- dispatch: float32 [128, 16, 20480], P('scen', None, 'gen')
- prices: float32 [128, 16, 256], P('scen')
- plan: float32 [16, 20480], P(None, 'gen')
All inputs are finite; a program needn't handle non-finite values. No bound on the sum of `block_map` on one device may be relied on, other than what follows from the above.
Results may differ from a plain program's by a relative error of at most 0.0003.
Values sent between devices are 32-bit elements; how exact they have to be, the bound alone decides.
No kernel may reach another device: no remote copies, remote signals or barrier semaphores. Data moves between devices by JAX's collectives and lax.ppermute only.
A program may use at most 128 MiB of HBM per device.

v0:
```python
import jax
import jax.numpy as jnp
from jax import lax
from jax.sharding import PartitionSpec as P

G = 20480
ITERS = 5


penalty = 2.0
centering = 0.5
epsilon = 1e-06


def local(
    zone_load,
    linear_cost,
    cost_diag,
    capacity,
    cost_tiles,
    coupling_tiles,
    block_map,
    zone_index,
    step_numer,
    step_denom,
):
    local_scen = zone_load.shape[0]
    periods = linear_cost.shape[0]
    zone_count = zone_load.shape[2]
    local_gen = capacity.shape[0]
    local_blocks = cost_tiles.shape[0]
    tile_width = cost_tiles.shape[2]
    gen_devices = lax.axis_size("gen")
    total_scen = local_scen * lax.axis_size("scen")
    row_count = local_scen * periods
    entries = float(total_scen * periods * G)
    coupling = coupling_tiles[0]
    block_mask = block_map[0].astype(jnp.float32)
    onehot = (zone_index[:, None] == jnp.arange(zone_count, dtype=jnp.int32)[None, :]).astype(
        jnp.float32
    )
    scen_ids = lax.axis_index("scen") * local_scen + jnp.arange(local_scen, dtype=jnp.int32)
    levels = 0.2 + 0.6 * (scen_ids.astype(jnp.float32) + 0.5) / total_scen
    dispatch = jnp.broadcast_to(levels[:, None, None] * capacity, (local_scen, periods, local_gen))
    low_dual = jnp.ones((local_scen, periods, local_gen), jnp.float32)
    high_dual = jnp.ones((local_scen, periods, local_gen), jnp.float32)
    prices = jnp.zeros((local_scen, periods, zone_count), jnp.float32)
    lowest = 0.02 * capacity
    highest = 0.98 * capacity
    plan = jnp.zeros((periods, local_gen), jnp.float32)
    for iteration in range(ITERS):
        step_size = step_numer[iteration].astype(jnp.float32) / step_denom[iteration].astype(
            jnp.float32
        )
        column_sums = lax.psum(jnp.sum(dispatch, axis=0), "scen")
        plan = column_sums / total_scen
        partial_value = jnp.dot(
            dispatch.reshape(row_count, local_gen),
            onehot,
            precision=lax.Precision.HIGHEST,
            preferred_element_type=jnp.float32,
        )
        totals = lax.psum(partial_value, "gen")
        imbalance = totals.reshape(local_scen, periods, zone_count) * (zone_count / G) - zone_load
        primal_local = jnp.sum(imbalance * imbalance) / gen_devices
        rounded = dispatch.astype(jnp.bfloat16).reshape(row_count, local_blocks, tile_width)
        cross_part = jnp.einsum(
            "rki,kij->rkj", rounded, coupling, preferred_element_type=jnp.float32
        )
        own_part = jnp.einsum(
            "rki,kij->rkj", rounded, cost_tiles, preferred_element_type=jnp.float32
        )
        products = (own_part + cross_part * block_mask[None, :, None]).reshape(
            local_scen, periods, local_gen
        )
        price_terms = jnp.dot(
            prices.reshape(row_count, zone_count),
            onehot.T,
            precision=lax.Precision.HIGHEST,
            preferred_element_type=jnp.float32,
        )
        residual = (
            cost_diag * dispatch
            + products
            + linear_cost
            + penalty * (dispatch - plan)
            + price_terms.reshape(local_scen, periods, local_gen)
            - low_dual
            + high_dual
        )
        gap_local = jnp.sum(dispatch * low_dual + (capacity - dispatch) * high_dual)
        dual_local = jnp.sum(residual * residual)
        stacked = jnp.stack([gap_local, dual_local, primal_local])
        summed = lax.psum(stacked, ("scen", "gen"))
        gap_sum = summed[0]
        dual_sq = summed[1]
        primal_sq = summed[2]
        target = centering * gap_sum / (2.0 * entries)
        dual_rms = jnp.sqrt(dual_sq / entries + epsilon)
        primal_rms = jnp.sqrt(primal_sq / float(total_scen * periods * zone_count) + epsilon)
        scaling = cost_diag + penalty + low_dual / dispatch + high_dual / (capacity - dispatch)
        updated = jnp.clip(
            dispatch - step_size * residual / (scaling * (1.0 + dual_rms)), lowest, highest
        )
        low_dual = low_dual + step_size * (target / updated - low_dual)
        high_dual = high_dual + step_size * (target / (capacity - updated) - high_dual)
        prices = prices + step_size * imbalance / (1.0 + primal_rms)
        dispatch = updated
    return (dispatch, prices, plan)


def solution(mesh):
    placed = (
        P("scen", None, None),
        P(None, "gen"),
        P("gen"),
        P("gen"),
        P("gen", None, None),
        P("scen", "gen", None, None),
        P("scen", "gen"),
        P("gen"),
        P(),
        P(),
    )
    return jax.shard_map(
        local,
        mesh=mesh,
        in_specs=placed,
        out_specs=(P("scen", None, "gen"), P("scen", None, None), P(None, "gen")),
        check_vma=False,
    )
```

profile of v0, /device:TPU:0, one launch (start us, length us, event | category | flops | bytes accessed | tf_op | source)
XLA Modules:
  0.0 921.3 jit_solution(15415761440046506945)
XLA Ops:
  9.6 3.9 fusion.16
  26.4 5.5 reshape.257
  31.9 2.9 fusion.66
  36.5 5.7 copy.38
  42.3 7.0 reshape.258
  52.3 71.3 %all-reduce.11.cloned.1.call-done = f32[16,5120]{1,0:T(8,128)} async-done(((f32[16,5120]{1,0:T(8,128)}), f32[16,5120]{1,0:T(8,128)}) %all-reduce.11.cloned.1.call-update) | async-done | bytes 327696 | tf_op jit(solution)/shard_map/psum | solution.py:55
  124.6 9.1 multiply_reduce_fusion.4
  135.1 40.0 %psum.107 = f32[3]{0:T(128)S(1)} all-reduce(f32[3]{0:T(128)S(1)} %pad_maximum_fusion), channel_id=1, replica_groups=mesh['scen'=8,'gen'=4] {'scen','gen'}, use_global_device_ids=true, to_apply=%region_6.0 | all-reduce | flops 3 | bytes 24 | tf_op jit(solution)/shard_map/psum | solution.py:94
  177.1 6.8 add_reduce_fusion.3
  187.0 3.9 fusion.14
  191.0 5.6 reshape.261
  196.6 2.9 fusion.63
  201.9 5.7 copy.41
  207.7 7.0 reshape.262
  214.9 8.1 all-reduce.17.cloned.1.call-done
  225.3 72.3 %all-reduce.15.cloned.1.call-done = f32[16,5120]{1,0:T(8,128)} async-done(((f32[16,5120]{1,0:T(8,128)}), f32[16,5120]{1,0:T(8,128)}) %all-reduce.15.cloned.1.call-update) | async-done | bytes 327696 | tf_op jit(solution)/shard_map/psum | solution.py:55
  298.7 11.3 %multiply_reduce_fusion.3 = (f32[]{:T(128)}, f32[16,16,5120]{2,1,0:T(8,128)}) fusion(f32[16,16,5120]{2,1,0:T(8,128)} %copy-done.1, f32[5120]{0:T(1024)S(1)} %copy-done.17, f32[]{:T(128)} %bitcast.14, f32[]{:T(128)} %bitcast, s32[5120]{0:T(1024)S(1)} %copy-done.23, f32[]{:T(128)} %bitcast.13, f32[16,16,256]{2,1,0:T(8,128)S(1)} %bitcast.123, ...), kind=kOutput, calls=%fused_computation.38 | convolution fusion | flops 4054253568 | bytes 16969744 | tf_op jit(solution)/shard_map/dot_general | solution.py:76
  311.5 39.5 %psum.110 = f32[3]{0:T(128)S(1)} all-reduce(f32[3]{0:T(128)S(1)} %pad_maximum_fusion.1), channel_id=1, replica_groups=mesh['scen'=8,'gen'=4] {'scen','gen'}, use_global_device_ids=true, to_apply=%region_13.14 | all-reduce | flops 3 | bytes 24 | tf_op jit(solution)/shard_map/psum | solution.py:94
  353.0 9.8 %add_reduce_fusion.2 = (f32[]{:T(128)}, f32[16,5120]{1,0:T(8,128)}, f32[16,16,5120]{2,1,0:T(8,128)S(1)}) fusion(f32[5120]{0:T(1024)S(1)} %copy-done.17, f32[]{:T(128)} %bitcast.24, f32[]{:T(128)} %bitcast.11, f32[16,16,5120]{2,1,0:T(8,128)} %copy-done.1, f32[]{:T(128)} %bitcast.14, f32[]{:T(128)} %bitcast, f32[]{:T(128)} %bitcast.20, ...), kind=kLoop, calls=%fused_computation.33 | loop fusion | flops 43171840 | bytes 16138264 | tf_op jit(solution)/shard_map/reduce_sum | solution.py:91
  365.9 3.9 fusion.12
  370.1 5.6 reshape.264
  375.7 2.9 fusion.60
  381.0 5.7 copy.44
  386.8 7.0 reshape.265
  393.9 8.0 all-reduce.21.cloned.1.call-done
  405.2 71.9 %all-reduce.19.cloned.1.call-done = f32[16,5120]{1,0:T(8,128)} async-done(((f32[16,5120]{1,0:T(8,128)}), f32[16,5120]{1,0:T(8,128)}) %all-reduce.19.cloned.1.call-update) | async-done | bytes 327696 | tf_op jit(solution)/shard_map/psum | solution.py:55
  478.1 13.2 %multiply_reduce_fusion.2 = (f32[]{:T(128)}, f32[16,16,5120]{2,1,0:T(8,128)}) fusion(f32[16,16,5120]{2,1,0:T(8,128)} %copy-done.4, f32[16,16,5120]{2,1,0:T(8,128)} %copy-done.1, f32[5120]{0:T(1024)S(1)} %copy-done.17, f32[]{:T(128)} %bitcast.24, f32[]{:T(128)} %bitcast.11, f32[]{:T(128)} %bitcast.14, f32[]{:T(128)} %bitcast, ...), kind=kOutput, calls=%fused_computation.32 | convolution fusion | flops 4065853440 | bytes 21950484 | tf_op jit(solution)/shard_map/dot_general | solution.py:76
  492.7 39.8 %psum.113 = f32[3]{0:T(128)S(1)} all-reduce(f32[3]{0:T(128)S(1)} %pad_maximum_fusion.2), channel_id=1, replica_groups=mesh['scen'=8,'gen'=4] {'scen','gen'}, use_global_device_ids=true, to_apply=%region_20.21 | all-reduce | flops 3 | bytes 24 | tf_op jit(solution)/shard_map/psum | solution.py:94
  534.5 14.1 %add_reduce_fusion.1 = (f32[]{:T(128)}, f32[16,5120]{1,0:T(8,128)}, f32[16,16,5120]{2,1,0:T(8,128)}, f32[16,16,5120]{2,1,0:T(8,128)}, f32[16,16,5120]{2,1,0:T(8,128)S(1)}) fusion(f32[5120]{0:T(1024)S(1)} %copy-done.17, f32[]{:T(128)} %bitcast.34, f32[]{:T(128)} %bitcast.21, f32[16,16,5120]{2,1,0:T(8,128)} %copy-done.4, f32[]{:T(128)} %bitcast.24, ...), kind=kLoop, calls=%fused_computation.27 | loop fusion | flops 54968320 | bytes 31866912 | tf_op jit(solution)/shard_map/reduce_sum | solution.py:91
  551.8 3.9 fusion.13
  556.2 5.6 reshape.267
  561.8 2.9 fusion.57
  567.2 5.7 copy.47
  572.9 7.0 reshape.268
  580.0 7.8 all-reduce.25.cloned.1.call-done
  590.1 73.0 %all-reduce.23.cloned.1.call-done = f32[16,5120]{1,0:T(8,128)} async-done(((f32[16,5120]{1,0:T(8,128)}), f32[16,5120]{1,0:T(8,128)}) %all-reduce.23.cloned.1.call-update) | async-done | bytes 327696 | tf_op jit(solution)/shard_map/psum | solution.py:55
  664.2 12.4 %multiply_reduce_fusion.1 = (f32[]{:T(128)}, f32[16,16,5120]{2,1,0:T(8,128)}) fusion(f32[16,16,5120]{2,1,0:T(8,128)} %get-tuple-element.13, f32[16,16,5120]{2,1,0:T(8,128)} %get-tuple-element.12, s32[5120]{0:T(1024)S(1)} %copy-done.23, f32[16,16,256]{2,1,0:T(8,128)S(1)} %get-tuple-element.19, f32[]{:T(128)} %bitcast.33, f32[]{:T(128)} %bitcast.21, ...), kind=kOutput, calls=%fused_computation.26 | convolution fusion | flops 4042588160 | bytes 27697164 | tf_op jit(solution)/shard_map/dot_general | solution.py:76
  677.9 39.7 %psum.116 = f32[3]{0:T(128)S(1)} all-reduce(f32[3]{0:T(128)S(1)} %pad_maximum_fusion.3), channel_id=1, replica_groups=mesh['scen'=8,'gen'=4] {'scen','gen'}, use_global_device_ids=true, to_apply=%region_27.28 | all-reduce | flops 3 | bytes 24 | tf_op jit(solution)/shard_map/psum | solution.py:94
  719.6 10.6 %add_reduce_fusion = (f32[]{:T(128)}, f32[16,5120]{1,0:T(8,128)}, f32[16,16,5120]{2,1,0:T(8,128)S(1)}) fusion(f32[5120]{0:T(1024)S(1)} %copy-done.17, f32[16,16,5120]{2,1,0:T(8,128)} %get-tuple-element.12, f32[]{:T(128)} %bitcast.44, f32[]{:T(128)} %bitcast.31, f32[16,16,5120]{2,1,0:T(8,128)} %get-tuple-element.13, f32[16,16,5120]{2,1,0:T(8,128)} %copy-done.2, ...), kind=kLoop, calls=%fused_computation.21 | loop fusion | flops 32686080 | bytes 26624016 | tf_op jit(solution)/shard_map/reduce_sum | solution.py:91
  733.3 3.9 fusion.15
  737.5 5.6 reshape.270
  748.4 5.7 copy.50
  754.2 7.0 reshape.271
  761.2 8.1 all-reduce.29.cloned.1.call-done
  773.5 71.1 %all-reduce.27.cloned.1.call-done = f32[16,5120]{1,0:T(8,128)} async-done(((f32[16,5120]{1,0:T(8,128)}), f32[16,5120]{1,0:T(8,128)}) %all-reduce.27.cloned.1.call-update) | async-done | bytes 327696 | tf_op jit(solution)/shard_map/psum | solution.py:55
  845.5 14.3 %multiply_reduce_fusion = (f32[]{:T(128)}, f32[16,16,5120]{2,1,0:T(8,128)}) fusion(f32[16,16,5120]{2,1,0:T(8,128)} %get-tuple-element.13, f32[16,16,5120]{2,1,0:T(8,128)} %copy-done.3, f32[5120]{0:T(1024)S(1)} %copy-done.17, f32[16,16,5120]{2,1,0:T(8,128)} %get-tuple-element.12, f32[]{:T(128)} %bitcast.44, f32[]{:T(128)} %bitcast.31, ...), kind=kOutput, calls=%fused_computation.20 | convolution fusion | flops 4054056960 | bytes 27193356 | tf_op jit(solution)/shard_map/dot_general | solution.py:76
  861.2 39.5 %psum.119 = f32[3]{0:T(128)S(1)} all-reduce(f32[3]{0:T(128)S(1)} %pad_maximum_fusion.4), channel_id=1, replica_groups=mesh['scen'=8,'gen'=4] {'scen','gen'}, use_global_device_ids=true, to_apply=%region_34.35 | all-reduce | flops 3 | bytes 24 | tf_op jit(solution)/shard_map/psum | solution.py:94
  902.7 10.7 %maximum_minimum_fusion = f32[16,16,5120]{2,1,0:T(8,128)} fusion(f32[16,16,5120]{2,1,0:T(8,128)} %copy-done.3, f32[16,16,5120]{2,1,0:T(8,128)} %get-tuple-element.59, f32[]{:T(128)} %bitcast.50, f32[]{:T(128)} %bitcast.41, f32[5120]{0:T(1024)S(1)} %copy-done.17, f32[5120]{0:T(1024)S(1)} %broadcast_add_fusion, f32[5120]{0:T(1024)S(1)} %get-tuple-element.25, ...), kind=kLoop, calls=%fused_computation.19 | loop fusion | flops 24903680 | bytes 26296336 | tf_op jit(solution)/shard_map/jit(clip)/min | solution.py:102
  (127 shorter events, 61.7 us)
Async XLA Ops:
  7.2 24.8 %copy-start = (bf16[20,256,256]{2,1,0:T(8,128)(2,1)S(1)}, bf16[20,256,256]{2,1,0:T(8,128)(2,1)}, u32[]{:S(2)}) copy-start(bf16[20,256,256]{2,1,0:T(8,128)(2,1)} %param.14) | copy-start | bytes 7864324
  7.2 2.5 copy-start.23
  7.2 42.1 %all-reduce.13.cloned.1.call-start = ((), (), s32[]{:S(2)}) async-start(), calls=%async_computation.1 | async-start | bytes 524288 | tf_op jit(solution)/shard_map/psum | solution.py:63
  9.0 4.7 copy-start.17
  9.0 7.9 copy-start.28
  9.0 7.9 copy-start.26
  9.0 11.8 %copy-start.27 = (s32[5]{0:T(128)S(1)}, s32[5]{0:T(128)}, u32[]{:S(2)}) copy-start(s32[5]{0:T(128)} %param.19) | copy-start | bytes 64
  9.0 15.6 %copy-start.25 = (f32[5120]{0:T(1024)S(1)}, f32[5120]{0:T(1024)}, u32[]{:S(2)}) copy-start(f32[5120]{0:T(1024)} %param.12) | copy-start | bytes 61444
  13.6 110.0 %all-reduce.11.cloned.1.call-start = ((), (), s32[]{:S(2)}) async-start(), calls=%async_computation | async-start | bytes 655360 | tf_op jit(solution)/shard_map/psum | solution.py:55
  14.6 208.5 %all-reduce.17.cloned.1.call-start = ((), (), s32[]{:S(2)}) async-start(), calls=%async_computation.3 | async-start | bytes 524288 | tf_op jit(solution)/shard_map/psum | solution.py:63
  31.9 2.9 copy-start.5
  31.9 3.6 copy-start.11
  42.3 8.7 copy-start.15
  50.2 0.7 copy-start.20
  183.8 3.1 copy-start.1
  191.0 106.7 %all-reduce.15.cloned.1.call-start = ((), (), s32[]{:S(2)}) async-start(), calls=%async_computation.2 | async-start | bytes 655360 | tf_op jit(solution)/shard_map/psum | solution.py:55
  196.6 2.9 copy-start.6
  196.6 3.6 copy-start.12
  207.7 91.0 %copy-start.21 = (f32[256,256]{1,0:T(8,128)S(1)}, f32[256,256]{1,0:T(8,128)}, u32[]{:S(2)}) copy-start(f32[256,256]{1,0:T(8,128)} %copy-done.20) | copy-start | bytes 786436
  214.7 187.2 %all-reduce.21.cloned.1.call-start = ((), (), s32[]{:S(2)}) async-start(), calls=%async_computation.5 | async-start | bytes 524288 | tf_op jit(solution)/shard_map/psum | solution.py:63
  362.8 3.1 copy-start.4
  369.8 107.2 %all-reduce.19.cloned.1.call-start = ((), (), s32[]{:S(2)}) async-start(), calls=%async_computation.4 | async-start | bytes 655360 | tf_op jit(solution)/shard_map/psum | solution.py:55
  375.7 2.9 copy-start.7
  375.7 3.6 copy-start.13
  386.8 16.1 %copy-start.18 = (f32[256,256]{1,0:T(8,128)S(1)}, f32[256,256]{1,0:T(8,128)}, u32[]{:S(2)}) copy-start(f32[256,256]{1,0:T(8,128)} %all-reduce.13.cloned.1.call-done) | copy-start | bytes 786436
  393.8 194.0 %all-reduce.25.cloned.1.call-start = ((), (), s32[]{:S(2)}) async-start(), calls=%async_computation.7 | async-start | bytes 524288 | tf_op jit(solution)/shard_map/psum | solution.py:63
  548.7 3.1 copy-start.2
  555.7 107.4 %all-reduce.23.cloned.1.call-start = ((), (), s32[]{:S(2)}) async-start(), calls=%async_computation.6 | async-start | bytes 655360 | tf_op jit(solution)/shard_map/psum | solution.py:55
  561.8 2.9 copy-start.8
  561.8 3.6 copy-start.14
  572.9 91.2 %copy-start.16 = (f32[256,256]{1,0:T(8,128)S(1)}, f32[256,256]{1,0:T(8,128)}, u32[]{:S(2)}) copy-start(f32[256,256]{1,0:T(8,128)} %all-reduce.21.cloned.1.call-done) | copy-start | bytes 786436
  580.0 189.3 %all-reduce.29.cloned.1.call-start = ((), (), s32[]{:S(2)}) async-start(), calls=%async_computation.9 | async-start | bytes 524288 | tf_op jit(solution)/shard_map/psum | solution.py:63
  730.2 3.1 copy-start.3
  737.2 107.3 %all-reduce.27.cloned.1.call-start = ((), (), s32[]{:S(2)}) async-start(), calls=%async_computation.8 | async-start | bytes 655360 | tf_op jit(solution)/shard_map/psum | solution.py:55
  743.1 2.9 copy-start.9
  743.1 3.6 copy-start.10
  845.5 14.3 %copy-start.24 = (f32[16,5120]{1,0:T(8,128)}, f32[16,5120]{1,0:T(8,128)S(1)}, u32[]{:S(2)}) copy-start(f32[16,5120]{1,0:T(8,128)S(1)} %broadcast_multiply_fusion) | copy-start | bytes 983044
  902.7 10.7 %copy-start.19 = (f32[256,256]{1,0:T(8,128)S(1)}, f32[256,256]{1,0:T(8,128)}, u32[]{:S(2)}) copy-start(f32[256,256]{1,0:T(8,128)} %all-reduce.29.cloned.1.call-done) | copy-start | bytes 786436
  902.7 10.7 %copy-start.22 = (f32[16,16,256]{2,1,0:T(8,128)S(1)}, f32[16,16,256]{2,1,0:T(8,128)}, u32[]{:S(2)}) copy-start(f32[16,16,256]{2,1,0:T(8,128)} %get-tuple-element.18) | copy-start | bytes 786436
Sparse Core Ops, SparseCore 0:
  13.7 35.0 all-reduce.12
  52.1 71.3 all-reduce.10
  191.1 31.9 all-reduce.16
  226.3 71.3 all-reduce.14
  370.0 31.8 all-reduce.20
  405.7 71.3 all-reduce.18
  555.8 31.9 all-reduce.24
  591.7 71.3 all-reduce.22
  737.4 31.9 all-reduce.28
  773.1 71.3 all-reduce.26
where the time goes:
time: 927 us; the launch traced here: 921 us
  waiting for transfers between devices  392 us (42%)
  blocking collectives  199 us (21%)
  local copies, waits for them, and re-layouts  108 us (12%)
  matrix products  99.4 us (11%)
  other arithmetic  87.8 us (9%)
  between operations  34.2 us (4%)
    psum x5, waiting for transfers between devices, local(): column_sums = lax.psum(jnp.sum(dispatch, axis=0), 'scen')  360 us
    psum x5, blocking collectives, local(): summed = lax.psum(stacked, ('scen', 'gen'))  199 us
    dot_general x5, matrix products, local(): jnp.dot(prices.reshape(row_count, zone_count), onehot.T, precision=lax.Pr...  60.4 us
    reduce_sum x5, other arithmetic, local(): gap_local = jnp.sum(dispatch * low_dual + (capacity - dispatch) * high_dual)  43.2 us
    reshape x5, local copies, waits for them, and re-layouts, local(): (own_part + cross_part * block_mask[None, :, None]).reshape(local_scen, p...  35 us
    psum x5, waiting for transfers between devices, local(): totals = lax.psum(partial_value, 'gen')  32 us
    add x5, local copies, waits for them, and re-layouts, local(): own_part + cross_part * block_mask[None, :, None]  28.7 us
    reshape x5, local copies, waits for them, and re-layouts, local(): dispatch.astype(jnp.bfloat16).reshape(row_count, local_blocks, tile_width)  27.8 us
  transfers between devices with their start and end apart: 10, of which 9 were waited for; matrix products, arithmetic and copies ran while one was open for 14% of the time, Pallas kernels for 0%

commit v1 on v0

v1 whole, which is shorter than its diff:
```python
import functools

import jax
import jax.numpy as jnp
import numpy as np
from jax import lax
from jax.experimental import pallas as pl
from jax.experimental.pallas import tpu as pltpu
from jax.sharding import PartitionSpec as P

PENALTY = 2.0
CENTERING = 0.5
EPSILON = 1e-06
LANES = 128

F32 = jnp.float32
BF16 = jnp.bfloat16
NT = (((1,), (1,)), ((), ()))
NN = (((1,), (0,)), ((), ()))


def dot(a, b, dims):
    return lax.dot_general(a, b, dims, preferred_element_type=F32)


def split(x):
    hi = x.astype(BF16)
    return hi, (x - hi.astype(F32)).astype(BF16)


def lane(row, i):
    return row[:, i : i + 1]


def zone_rows(zone_ref, cols, size, zones):
    ids = lax.broadcasted_iota(jnp.int32, (zones, size), 0)
    return (ids == zone_ref[:, cols]).astype(BF16)


def total(x):
    return jnp.sum(jnp.sum(x, axis=1, keepdims=True), axis=0, keepdims=True)


def stage(body, n_small, n_large, n_small_out, n_large_out, extra):
    def kernel(*refs):
        refs = list(refs)

        def take(n):
            out = refs[:n]
            del refs[:n]
            return out

        first, small, large = take(extra), take(n_small), take(n_large)
        small_out, large_out = take(n_small_out), take(n_large_out)
        held, made = take(n_small), take(n_small_out)
        in_sems, out_sems = take(2)
        loads = [pltpu.make_async_copy(a, b, in_sems.at[j]) for j, (a, b) in enumerate(zip(small, held))]
        for copy in loads:
            copy.start()

        def ready():
            for copy in loads:
                copy.wait()

        finish = body(ready, first, held, large, made, large_out, refs)
        stores = [pltpu.make_async_copy(b, a, out_sems.at[j]) for j, (a, b) in enumerate(zip(small_out, made))]
        for copy in stores:
            copy.start()
        finish()
        for copy in stores:
            copy.wait()

    return kernel


def staged_call(
    body, first, small, large, small_out, large_out, scratch, name, cost=None, aliases=None
):
    dma = pltpu.SemaphoreType.DMA
    hbm = pl.BlockSpec(memory_space=pl.ANY)
    begin = len(first) + len(small)
    alias = {begin + a: len(small_out) + b for a, b in (aliases or {}).items()}
    return pl.pallas_call(
        stage(body, len(small), len(large), len(small_out), len(large_out), len(first)),
        in_specs=[pl.BlockSpec(memory_space=pltpu.SMEM)] * len(first) + [hbm] * (len(small) + len(large)),
        out_specs=[hbm] * (len(small_out) + len(large_out)),
        out_shape=small_out + large_out,
        scratch_shapes=[pltpu.VMEM(v.shape, v.dtype) for v in small + small_out]
        + [dma((max(1, len(small)),)), dma((max(1, len(small_out)),))]
        + scratch,
        input_output_aliases=alias,
        compiler_params=params(60),
        cost_estimate=cost,
        name=name,
    )(*first, *small, *large)


def lanes(c, width, t=0, size=None):
    return pl.ds(pl.multiple_of(c * width + t, LANES), width if size is None else size)


def first_body(dims, ready, first, small, large, made, large_out, scratch):
    (mask_ref,) = first
    level_ref, load_ref, lin_ref, diag_ref, cap_ref, zone_ref = small
    cost_in, coup_in = large
    base_ref, pack_ref = made
    sums, capz, cost, coup, sems = scratch
    ns, periods = dims.local_scen, dims.periods
    zones = load_ref.shape[1]
    chunks, per, tile = cost.shape[:3]

    def copies(c):
        return [
            pltpu.make_async_copy(source.at[c], target.at[c], sems.at[j, c])
            for j, (source, target) in enumerate([(cost_in, cost), (coup_in, coup)])
        ]

    @pl.loop(0, chunks)
    def _(c):
        for copy in copies(c):
            copy.start()

    ready()
    sums[...] = jnp.zeros_like(sums)
    capz[...] = jnp.zeros_like(capz)
    load = jnp.zeros((periods, zones), F32)
    weighted = jnp.zeros((periods, zones), F32)
    for s in range(ns):
        part = load_ref[s * periods : (s + 1) * periods, :]
        load += part * part
        weighted += level_ref[s : s + 1, 0:1] * part

    @pl.loop(0, chunks)
    def _(c):
        for copy in copies(c):
            copy.wait()
        levels = level_ref[:, 0:1]
        dual = jnp.zeros((1, tile), F32)
        caps = jnp.zeros((1, tile), F32)
        for t in range(per):
            cols = lanes(c, per * tile, t * tile, tile)
            cap = cap_ref[:, cols]
            lin = lin_ref[:, cols]
            dispatch = levels * cap
            rounded = dispatch.astype(BF16)
            on = mask_ref[c * per + t].astype(F32).astype(BF16)
            products = dot(rounded, cost[c, t], NN) + dot(rounded, coup[c, t] * on, NN)
            base = (
                (diag_ref[:, cols] + PENALTY) * dispatch + products - PENALTY * dims.mean_level * cap
            )
            base_ref[:, cols] = base
            dual += (
                periods * jnp.sum(base * base, axis=0, keepdims=True)
                + 2.0
                * jnp.sum(base, axis=0, keepdims=True)
                * jnp.sum(lin, axis=0, keepdims=True)
                + ns * jnp.sum(lin * lin, axis=0, keepdims=True)
            )
            caps += cap
            hi = cap.astype(BF16)
            rest = cap - hi.astype(F32)
            mid = rest.astype(BF16)
            low = (rest - mid.astype(F32)).astype(BF16)
            rows = jnp.concatenate(
                [jnp.broadcast_to(v.astype(F32), (8, tile)) for v in (hi, mid, low)], axis=0
            ).astype(BF16)
            capz[...] += dot(rows, zone_rows(zone_ref, cols, tile, zones), NT)
        sums[0:1, :] += dual
        sums[1:2, :] += caps

    weighted = jnp.sum(weighted, axis=0, keepdims=True) * (1.0 / dims.gen_devices)
    zcap = (capz[0:1, :] + capz[8:9, :] + capz[16:17, :]) * (1.0 / dims.scen_devices)
    dual_all = total(sums[0:1, :])
    gap_all = total(sums[1:2, :]) * float(ns * periods)
    load_all = total(load) * (1.0 / dims.gen_devices)
    ids = lax.broadcasted_iota(jnp.int32, (1, LANES), 1)
    row = jnp.where(ids == 0, gap_all, jnp.where(ids == 1, dual_all, load_all))
    parts = [row]
    for source in (zcap, weighted):
        parts += [source[:, i * LANES : (i + 1) * LANES] for i in range(zones // LANES)]
    parts.append(jnp.zeros((pack_ref.shape[1] - len(parts), LANES), F32))
    pack_ref[...] = jnp.broadcast_to(jnp.concatenate(parts, axis=0)[None], pack_ref.shape)
    return lambda: None


def scalars(dims, gap, dual, primal, size):
    target = CENTERING * gap / (2.0 * dims.entries)
    rms = jnp.sqrt(jnp.maximum(dual, 0.0) / dims.entries + EPSILON)
    primal_rms = jnp.sqrt(jnp.maximum(primal, 0.0) / dims.zone_entries + EPSILON)
    return size / (1.0 + rms), size / (1.0 + primal_rms), size * target


def keep(coef, before, k, move, shift, size):
    coef[0:8, :] = jnp.broadcast_to(move, (8, LANES))
    for i in range(k + 1):
        old = 1.0 if before is None else before[8 + 8 * i : 16 + 8 * i, :]
        coef[8 + 8 * i : 16 + 8 * i, :] = jnp.broadcast_to((1.0 - size) * old, (8, LANES))
    coef[16 + 8 * k : 24 + 8 * k, :] = jnp.broadcast_to(shift, (8, LANES))


def zone_sums(block, zone_ref, c, tot_ref):
    width, zones = block.shape[1], tot_ref.shape[1]
    tile = zones if width % zones == 0 else width
    for t in range(width // tile):
        hi, lo = split(block[:, t * tile : (t + 1) * tile])
        pick = zone_rows(zone_ref, lanes(c, width, t * tile, tile), tile, zones)
        tot_ref[...] += dot(hi, pick, NT) + dot(lo, pick, NT)


def start_body(dims, ready, first, small, large, made, large_out, scratch):
    recv_ref, size_ref, level_ref, load_ref, base_ref, lin_ref, diag_ref, cap_ref, zone_ref = small
    col_ref, price_ref, tot_ref, coef_ref = made
    (disp_ref,) = large_out
    buf, sems = scratch
    ns, periods = dims.local_scen, dims.periods
    zones = load_ref.shape[1]
    chunks, width = buf.shape[0], buf.shape[2]
    ready()
    got = jnp.sum(recv_ref[...], axis=0)
    n = zones // LANES
    zcap = jnp.concatenate([got[1 + i : 2 + i] for i in range(n)], axis=1)
    weighted = jnp.concatenate([got[1 + n + i : 2 + n + i] for i in range(n)], axis=1)
    scaled = zcap * dims.zone_scale
    primal = total(scaled * (dims.level_sq * periods * scaled - 2.0 * weighted)) + lane(got[0:1], 2)
    size = size_ref[0, 0:1, 0:1]
    move, price, shift = scalars(dims, lane(got[0:1], 0), lane(got[0:1], 1), primal, size)
    keep(coef_ref, None, 0, move, shift, size)
    for s in range(ns):
        rows = slice(s * periods, (s + 1) * periods)
        price_ref[rows, :] = price * (level_ref[s : s + 1, 0:1] * scaled - load_ref[rows, :])
    tot_ref[...] = jnp.zeros_like(tot_ref)

    @pl.loop(0, chunks)
    def _(c):
        move = coef_ref[0:1, :]
        for t in range(width // LANES):
            cols = slice(t * LANES, (t + 1) * LANES)
            here = lanes(c, width, t * LANES, LANES)
            cap, stiff, lin = cap_ref[:, here], diag_ref[:, here] + PENALTY, lin_ref[:, here]
            lowest, highest = 0.02 * cap, 0.98 * cap
            acc = jnp.zeros((periods, LANES), F32)
            dispatch = level_ref[:, 0:1] * cap
            weight = move / (stiff + 1.0 / dispatch + 1.0 / (cap - dispatch))
            base = base_ref[:, here]
            for s in range(ns):
                one = slice(s, s + 1)
                new = dispatch[one] - weight[one] * (base[one] + lin)
                new = jnp.minimum(jnp.maximum(new, lowest), highest)
                buf[c, s * periods : (s + 1) * periods, cols] = new
                acc += new
            col_ref[c * (width // LANES) + t] = acc
        pltpu.make_async_copy(buf.at[c], disp_ref.at[c], sems.at[c]).start()
        zone_sums(buf.at[c], zone_ref, c, tot_ref)

    def finish():
        @pl.loop(0, chunks)
        def _(c):
            pltpu.make_async_copy(buf.at[c], disp_ref.at[c], sems.at[c]).wait()

    return finish


def update_body(dims, k, last, ready, first, small, large, made, large_out, scratch):
    recv_ref, size_ref, coef_in, price_in, imb_ref, plan_ref, cap_ref, zone_ref = small
    if last:
        price_ref, plan_out = made
    else:
        price_ref, col_ref, tot_ref, coef_ref = made
    (disp_out,) = large_out
    disp, resid, weight, step_ref, sems, out_sems = scratch
    ns, periods = dims.local_scen, dims.periods
    chunks, width = disp.shape[0], disp.shape[2]
    moves = list(zip(large, (disp, resid, weight)))

    def in_copies(c):
        return [
            pltpu.make_async_copy(source.at[c], target.at[c], sems.at[j, c])
            for j, (source, target) in enumerate(moves)
        ]

    @pl.loop(0, chunks)
    def _(c):
        for copy in in_copies(c):
            copy.start()

    ready()
    got = jnp.sum(recv_ref[...], axis=0)
    size = size_ref[k, 0:1, 0:1]
    move, price, shift = scalars(dims, lane(got, 0), lane(got, 1), lane(got, 2), size)
    step_ref[...] = jnp.broadcast_to(move, step_ref.shape)
    price_ref[...] = price_in[...] + price * imb_ref[...]
    if last:
        for t in range(plan_ref.shape[0]):
            plan_out[:, t * LANES : (t + 1) * LANES] = plan_ref[t] * (1.0 / dims.total_scen)
    else:
        keep(coef_ref, coef_in, k, move, shift, size)
        tot_ref[...] = jnp.zeros_like(tot_ref)

    def out_copy(c):
        target = disp_out.at[:, lanes(c, width)] if last else disp_out.at[c]
        return pltpu.make_async_copy(disp.at[c], target, out_sems.at[c])

    @pl.loop(0, chunks)
    def _(c):
        for copy in in_copies(c):
            copy.wait()
        move = step_ref[0:1, :]
        for t in range(width // LANES):
            cols = slice(t * LANES, (t + 1) * LANES)
            cap = cap_ref[:, lanes(c, width, t * LANES, LANES)]
            lowest, highest = 0.02 * cap, 0.98 * cap
            pull = plan_ref[c * (width // LANES) + t] * (PENALTY / dims.total_scen)
            acc = jnp.zeros((periods, LANES), F32)
            for s in range(ns):
                rows = slice(s * periods, (s + 1) * periods)
                new = disp[c, rows, cols] - move * (resid[c, rows, cols] - pull) * weight[c, rows, cols]
                new = jnp.minimum(jnp.maximum(new, lowest), highest)
                disp[c, rows, cols] = new
                acc += new
            if not last:
                col_ref[c * (width // LANES) + t] = acc
        out_copy(c).start()
        if not last:
            zone_sums(disp.at[c], zone_ref, c, tot_ref)

    def finish():
        @pl.loop(0, chunks)
        def _(c):
            out_copy(c).wait()

    return finish


def hidden_body(dims, k, last, begin, count, ready, first, small, large, made, large_out, scratch):
    (mask_ref,) = first
    coef_ref, price_ref, part_in, lin_ref, diag_ref, cap_ref, zone_ref = small
    past, cost_in, coup_in = large[:k], large[k], large[k + 1]
    col_ref, part_ref = made
    price_hi, price_lo, sums = scratch[:3]
    disps = scratch[3 : 3 + k]
    resid, weight, cost, coup, sems, out_sems = scratch[3 + k :]
    disp = disps[-1]
    ns, periods = dims.local_scen, dims.periods
    width = disp.shape[2]
    tile, zones = cost.shape[2], price_ref.shape[1]
    per = width // tile

    moves = [(cost_in, cost), (coup_in, coup)] + list(zip(past, disps))
    outs = list(zip((resid, weight), large_out))

    def in_copies(c):
        return [
            pltpu.make_async_copy(source.at[begin + c], target.at[c], sems.at[j, c])
            for j, (source, target) in enumerate(moves)
        ]

    def out_copies(c):
        return [
            pltpu.make_async_copy(source.at[c], target.at[begin + c], out_sems.at[j, c])
            for j, (source, target) in enumerate(outs)
        ]

    @pl.loop(0, count)
    def _(c):
        for copy in in_copies(c):
            copy.start()

    ready()
    hi, lo = split(price_ref[...])
    price_hi[...] = hi
    price_lo[...] = lo
    sums[...] = jnp.zeros_like(sums)

    @pl.loop(0, count)
    def _(c):
        for copy in in_copies(c):
            copy.wait()
        kept = coef_ref[8:9, :]
        shifts = [coef_ref[16 + 8 * i : 17 + 8 * i, :] for i in range(k)]
        gap = jnp.zeros((periods, LANES), F32)
        square = jnp.zeros((periods, LANES), F32)
        for t in range(per):
            cols = slice(t * tile, (t + 1) * tile)
            hi = disp[c, :, cols].astype(BF16)
            pick = zone_rows(zone_ref, lanes(begin + c, width, t * tile, tile), tile, zones)
            on = mask_ref[(begin + c) * per + t].astype(F32).astype(BF16)
            resid[c, :, cols] = (
                dot(hi, cost[c, t], NN)
                + dot(hi, coup[c, t] * on, NN)
                + dot(price_hi[...], pick, NN)
                + dot(price_lo[...], pick, NN)
            )
            for u in range(tile // LANES):
                cols = slice(t * tile + u * LANES, t * tile + (u + 1) * LANES)
                here = lanes(begin + c, width, t * tile + u * LANES, LANES)
                cap, stiff, lin = cap_ref[:, here], diag_ref[:, here] + PENALTY, lin_ref[:, here]
                acc = jnp.zeros((periods, LANES), F32)
                for s in range(ns):
                    rows = slice(s * periods, (s + 1) * periods)
                    low, high = kept, kept
                    for shift, source in zip(shifts, disps):
                        d = source[c, rows, cols]
                        e = cap - d
                        q = 1.0 / (d * e)
                        move = shift * q
                        low = low + move * e
                        high = high + move * d
                    weight[c, rows, cols] = 1.0 / (stiff + (low * e + high * d) * q)
                    a = stiff * d + resid[c, rows, cols] + lin - low + high
                    resid[c, rows, cols] = a
                    acc += a
                    square += a * a
                    if not last:
                        gap += low * d + high * e
                col_ref[c * (width // LANES) + t * (tile // LANES) + u] = acc
        sums[0] += gap
        sums[1] += square
        for copy in out_copies(c):
            copy.start()

    ids = lax.broadcasted_iota(jnp.int32, (8, LANES), 1)
    part_ref[...] = part_in[...] + jnp.where(
        ids == 0, total(sums[0]), jnp.where(ids == 1, total(sums[1]), 0.0)
    )

    def finish():
        @pl.loop(0, count)
        def _(c):
            for copy in out_copies(c):
                copy.wait()

    return finish


def piece_kernel(recv_ref, out_ref):
    out_ref[...] = jnp.broadcast_to(jnp.sum(recv_ref[...], axis=0, keepdims=True), out_ref.shape)


def imbalance_kernel(scale, share, near_ref, far_ref, load_ref, imb_ref, part_ref):
    imb = (near_ref[...] + far_ref[...]) * scale - load_ref[...]
    imb_ref[...] = imb
    part_ref[...] = jnp.broadcast_to(total(imb * imb) * share, part_ref.shape)


def pack_body(dims, ready, first, small, large, made, large_out, scratch):
    plan_ref, part_ref, primal_ref = small[:3]
    (out_ref,) = made
    ready()
    cross = jnp.zeros(plan_ref.shape[1:], F32)
    offset = 0
    for col_ref in small[3:]:
        for t in range(col_ref.shape[0]):
            plan = plan_ref[offset + t] * (1.0 / dims.total_scen)
            cross += plan * (PENALTY * dims.local_scen * plan - 2.0 * col_ref[t])
        offset += col_ref.shape[0]
    row = part_ref[0:1, :]
    ids = lax.broadcasted_iota(jnp.int32, (1, LANES), 1)
    row = jnp.where(ids == 1, row + PENALTY * total(cross), row)
    row = jnp.where(ids == 2, primal_ref[0:1, :], row)
    out_ref[...] = jnp.broadcast_to(row[None], out_ref.shape)
    return lambda: None


class Dims:
    pass


def params(limit):
    return pltpu.CompilerParams(vmem_limit_bytes=limit << 20)


def estimate(flops, size):
    return pl.CostEstimate(flops=flops, bytes_accessed=size, transcendentals=0)


def divisor(n, most):
    return max(d for d in range(1, most + 1) if n % d == 0)


def local(
    zone_load, linear_cost, cost_diag, capacity, cost_tiles, coupling_tiles, block_map, zone_index,
    step_numer, step_denom,
):
    local_scen, periods, zones = zone_load.shape
    local_gen = capacity.shape[0]
    blocks, tile = cost_tiles.shape[0], cost_tiles.shape[2]
    iters = step_numer.shape[0]
    scen_devices, gen_devices = lax.axis_size("scen"), lax.axis_size("gen")
    devices = scen_devices * gen_devices
    rows = local_scen * periods
    gens = local_gen * gen_devices
    total_scen = local_scen * scen_devices
    all_levels = 0.2 + 0.6 * (np.arange(total_scen) + 0.5) / total_scen

    dims = Dims()
    dims.local_scen, dims.periods = local_scen, periods
    dims.scen_devices, dims.gen_devices = scen_devices, gen_devices
    dims.total_scen = total_scen
    dims.mean_level = float(all_levels.mean())
    dims.level_sq = float((all_levels**2).sum())
    dims.entries = float(total_scen * periods * gens)
    dims.zone_entries = float(total_scen * periods * zones)
    dims.zone_scale = zones / gens

    load = zone_load.reshape(rows, zones)
    diag, cap, zone = (v.reshape(1, local_gen) for v in (cost_diag, capacity, zone_index))
    mask = block_map.reshape(blocks)
    sizes = step_numer.astype(F32) / step_denom.astype(F32)
    sizes = lax.optimization_barrier(jnp.broadcast_to(sizes[:, None, None], (iters, 8, LANES)))
    scen_ids = lax.axis_index("scen") * local_scen + jnp.arange(local_scen, dtype=jnp.int32)
    levels = 0.2 + 0.6 * (scen_ids.astype(F32) + 0.5) / total_scen
    levels = jnp.broadcast_to(levels[:, None], (local_scen, LANES))

    shape = jax.ShapeDtypeStruct
    dma = pltpu.SemaphoreType.DMA

    per = divisor(blocks, 2)
    width = per * tile
    chunks = blocks // per
    lane_tiles = local_gen // LANES

    cost_c = cost_tiles.reshape(chunks, per, tile, tile)
    coup_c = coupling_tiles.reshape(chunks, per, tile, tile)
    state = shape((chunks, rows, width), F32)
    buffer = pltpu.VMEM((chunks, rows, width), F32)
    part_shape = shape((8, LANES), F32)
    plan_shape = shape((periods, local_gen), F32)
    vector = [linear_cost, diag, cap, zone]
    col_shape = shape((lane_tiles, periods, LANES), F32)
    coef_shape = shape((16 + 8 * iters, LANES), F32)
    grid_shape = shape((rows, zones), F32)

    def exchange(x):
        return lax.all_to_all(x, ("scen", "gen"), 0, 0)

    pack_rows = -(-(1 + 2 * (zones // LANES)) // 8) * 8
    tiles = pltpu.VMEM((chunks, per, tile, tile), BF16)
    base, packed = staged_call(
        functools.partial(first_body, dims), [mask], [levels, load] + vector, [cost_c, coup_c],
        [shape((local_scen, local_gen), F32), shape((devices, pack_rows, LANES), F32)], [],
        [
            pltpu.VMEM((8, tile), F32), pltpu.VMEM((24, zones), F32), tiles, tiles,
            dma((2, chunks)),
        ],
        "first",
    )
    recv = exchange(packed)

    col_sums, prices, totals, coef, dispatch = staged_call(
        functools.partial(start_body, dims), [], [recv, sizes, levels, load, base] + vector, [],
        [col_shape, grid_shape, grid_shape, coef_shape], [state], [buffer, dma((chunks,))],
        "start",
    )

    past = [dispatch]
    nothing = lax.optimization_barrier(jnp.zeros((8, LANES), F32))
    odd = lax.axis_index("gen") % 2
    pieces = col_shape.shape[0] * periods // 8
    padded = -(-pieces // scen_devices) * scen_devices
    half_rows = rows // 2
    my_load = lax.dynamic_slice_in_dim(load, odd * half_rows, half_rows, 0)
    swap = [(i, i ^ 1) for i in range(gen_devices)]
    first_half = chunks // 2
    parts = [(0, first_half), (first_half, chunks - first_half)] if first_half else [(0, chunks)]

    for k in range(1, iters):
        last = k == iters - 1
        flat = col_sums.reshape(pieces, 8, LANES)
        if padded != pieces:
            flat = jnp.pad(flat, ((0, padded - pieces), (0, 0), (0, 0)))
        flat = flat.reshape(scen_devices, padded // scen_devices, 8, LANES)
        got = lax.all_to_all(flat, "scen", 0, 0)
        other = lax.ppermute(totals, "gen", swap)

        cols = []
        resid = weight = None
        partial = nothing
        for part, (begin, count) in enumerate(parts):
            part_buffer = pltpu.VMEM((count, rows, width), F32)
            weights = pltpu.VMEM((count, per, tile, tile), BF16)
            carry = [resid, weight] if part else []
            col_k, partial, resid, weight = staged_call(
                functools.partial(hidden_body, dims, k, last, begin, count),
                [mask], [coef, prices, partial] + vector, [*past, cost_c, coup_c, *carry],
                [shape((count * width // LANES, periods, LANES), F32), part_shape], [state, state],
                [
                    pltpu.VMEM((rows, zones), BF16), pltpu.VMEM((rows, zones), BF16),
                    pltpu.VMEM((2, periods, LANES), F32),
                ] + [part_buffer] * (k + 2) + [weights, weights, dma((k + 2, count)), dma((2, count))],
                "hidden",
                estimate(count * 24 * rows * tile * tile, count * 8 * rows * width * 4),
                {k + 2 + j: j for j in range(len(carry))},
            )
            cols.append(col_k)
            if part == 0:
                got, partial = lax.optimization_barrier((got, partial))
                piece = pl.pallas_call(
                    piece_kernel, out_shape=shape(got.shape, F32), compiler_params=params(4), name="piece"
                )(got)
                piece, partial = lax.optimization_barrier((piece, partial))
                gathered = lax.all_to_all(piece, "scen", 0, 0)

                totals = totals + other
                near = lax.dynamic_slice_in_dim(totals, odd * half_rows, half_rows, 0)
                far = jnp.zeros_like(near)
                bit = 2
                while bit < gen_devices:
                    if bit > 2:
                        near = near + far
                    far = lax.ppermute(near, "gen", [(i, i ^ bit) for i in range(gen_devices)])
                    bit *= 2

        far, partial = lax.optimization_barrier((far, partial))
        plan = gathered.reshape(padded, 8, LANES)[:pieces].reshape(lane_tiles, periods, LANES)
        mine, primal = pl.pallas_call(
            functools.partial(imbalance_kernel, dims.zone_scale, 2.0 / gen_devices),
            out_shape=[shape((half_rows, zones), F32), shape((8, LANES), F32)],
            compiler_params=params(4),
            name="imbalance",
        )(near, far, my_load)
        other = lax.ppermute(mine, "gen", swap)
        imbalance = jnp.where(
            odd == 0, jnp.concatenate([mine, other]), jnp.concatenate([other, mine])
        )

        (packed,) = staged_call(
            functools.partial(pack_body, dims), [], [plan, partial, primal, *cols], [],
            [shape((devices, 1, LANES), F32)], [], [], "pack",
        )
        recv = exchange(packed)

        small = [recv, sizes, coef, prices, imbalance, plan, cap, zone]
        large = [dispatch, resid, weight]
        scratch = [buffer] * 3 + [pltpu.VMEM((8, LANES), F32), dma((3, chunks)), dma((chunks,))]
        cost = estimate(rows * local_gen * 8, rows * local_gen * 16)
        body = functools.partial(update_body, dims, k, last)
        if last:
            prices, plan, dispatch = staged_call(
                body, [], small, large, [grid_shape, plan_shape], [shape((rows, local_gen), F32)],
                scratch, "update", cost,
            )
        else:
            prices, col_sums, totals, coef, dispatch = staged_call(
                body, [], small, large, [grid_shape, col_shape, grid_shape, coef_shape], [state],
                scratch, "update", cost,
            )
            past.append(dispatch)

    return (
        dispatch.reshape(local_scen, periods, local_gen),
        prices.reshape(local_scen, periods, zones),
        plan,
    )


def solution(mesh):
    placed = (
        P("scen", None, None),
        P(None, "gen"),
        P("gen"),
        P("gen"),
        P("gen", None, None),
        P("scen", "gen", None, None),
        P("scen", "gen"),
        P("gen"),
        P(),
        P(),
    )
    return jax.shard_map(
        local,
        mesh=mesh,
        in_specs=placed,
        out_specs=(P("scen", None, "gen"), P("scen", None, None), P(None, "gen")),
        check_vma=False,
    )
```

time: 927 us -> 252 us (0.27)
  waiting for transfers between devices: 392 us -> 42.5 us
  blocking collectives: 199 us -> 0 us
  Pallas kernels: 0 us -> 131 us
  matrix products: 99.4 us -> 0 us
  local copies, waits for them, and re-layouts: 108 us -> 10.2 us
  other arithmetic: 87.8 us -> 3.04 us
  starting transfers between devices: 1.77 us -> 62.7 us
  between operations: 34.2 us -> 1.32 us
    psum x10 -> x0, waiting for transfers between devices: 392 us -> none  [the longest x5 360 us: local(): column_sums = lax.psum(jnp.sum(dispatch, axis=0), 'scen')]
    psum x5 -> x0, blocking collectives: 199 us -> none  [local(): summed = lax.psum(stacked, ('scen', 'gen'))]
    pallas_call x0 -> x26, Pallas kernels: none -> 131 us  [the longest x18 127 us: staged_call(): pl.pallas_call(stage(body, len(small), len(large), len(small_out), len(la...]
    dot_general x20 -> x0, matrix products: 99.4 us -> none  [the longest x5 60.4 us: local(): jnp.dot(prices.reshape(row_count, zone_count), onehot.T, precision=lax.Pr...]
    reshape x10 -> x0, local copies, waits for them, and re-layouts: 62.8 us -> none  [the longest x5 35 us: local(): (own_part + cross_part * block_mask[None, :, None]).reshape(local_scen, p...]
    all_to_all x0 -> x13, starting transfers between devices: none -> 59.9 us  [the longest x5 28.5 us: exchange(): return lax.all_to_all(x, ('scen', 'gen'), 0, 0)]
    reduce_sum x10 -> x0, other arithmetic: 47.8 us -> none  [the longest x5 43.2 us: local(): gap_local = jnp.sum(dispatch * low_dual + (capacity - dispatch) * high_dual)]
    all_to_all x0 -> x13, waiting for transfers between devices: none -> 42.5 us  [the longest x5 33.2 us: exchange(): return lax.all_to_all(x, ('scen', 'gen'), 0, 0)]
  transfers between devices with their start and end apart: 10 -> 25, of which waited for: 9 -> 12; matrix products, arithmetic and copies ran while one was open for 14% -> 2% of each run, Pallas kernels for 0% -> 32%
where the time goes in v1:
time: 252 us; the launch traced here: 251 us
  Pallas kernels  131 us (52%)
  starting transfers between devices  62.7 us (25%)
  waiting for transfers between devices  42.5 us (17%)
  local copies, waits for them, and re-layouts  10.2 us (4%)
  other arithmetic  3.04 us (1%)
    pallas_call x18, Pallas kernels, staged_call(): pl.pallas_call(stage(body, len(small), len(large), len(small_out), len(la...  127 us
    all_to_all x5, waiting for transfers between devices, exchange(): return lax.all_to_all(x, ('scen', 'gen'), 0, 0)  33.2 us
    all_to_all x5, starting transfers between devices, exchange(): return lax.all_to_all(x, ('scen', 'gen'), 0, 0)  28.5 us
    all_to_all x4, starting transfers between devices, local(): gathered = lax.all_to_all(piece, 'scen', 0, 0)  17.7 us
    all_to_all x4, starting transfers between devices, local(): got = lax.all_to_all(flat, 'scen', 0, 0)  13.8 us
    unnamed x40, local copies, waits for them, and re-layouts  8.29 us
    all_to_all x4, waiting for transfers between devices, local(): got = lax.all_to_all(flat, 'scen', 0, 0)  5.83 us
  transfers between devices with their start and end apart: 25, of which 12 were waited for; matrix products, arithmetic and copies ran while one was open for 2% of the time, Pallas kernels for 32%

profile of v1, /device:TPU:0, one launch (start us, length us, event | category | flops | bytes accessed | tf_op | source)
XLA Modules:
  0.0 250.7 jit_solution(17117729842361799073)
XLA Ops:
  1.3 6.1 %first.1 = (f32[16,5120]{1,0:T(8,128)}, f32[32,8,128]{2,1,0:T(8,128)}) custom-call(s32[20]{0:T(128)} %bitcast.88, f32[16,128]{1,0:T(8,128)} %broadcast_in_dim.6.refs_1_.refs_2_, f32[256,256]{1,0:T(8,128)} %bitcast.81, f32[16,5120]{1,0:T(8,128)} %refs_4_.15, f32[1,5120]{1,0:T(1,128)} %bitcast.71, f32[1,5120]{1,0:T(1,128)} %bitcast.35, s32[1,5120]{1,0:T(1,128)} %bitcast.49, ...), custom_call_target="tpu_custom_call" | custom-call | tf_op jit(solution)/shard_map/first/pallas_call | solution.py:83
  7.4 7.3 %all-to-all-start = ((f32[32,8,128]{2,1,0:T(8,128)}), f32[32,8,128]{2,1,0:T(8,128)S(1)}, u32[]{:S(2)}, u32[]{:S(2)}) async-start(f32[32,8,128]{2,1,0:T(8,128)} %get-tuple-element.92), calls=%async_computation | async-start | bytes 262144 | tf_op jit(solution)/shard_map/all_to_all | solution.py:534
  15.4 7.5 %all-to-all-done.refs_0_ = f32[32,8,128]{2,1,0:T(8,128)S(1)} async-done(((f32[32,8,128]{2,1,0:T(8,128)}), f32[32,8,128]{2,1,0:T(8,128)S(1)}, u32[]{:S(2)}, u32[]{:S(2)}) %all-to-all-start) | async-done | bytes 131104 | tf_op jit(solution)/shard_map/all_to_all | solution.py:534
  23.6 7.2 %start.1 = (f32[40,16,128]{2,1,0:T(8,128)}, f32[256,256]{1,0:T(8,128)}, f32[256,256]{1,0:T(8,128)}, f32[56,128]{1,0:T(8,128)}, f32[10,256,512]{2,1,0:T(8,128)}) custom-call(f32[32,8,128]{2,1,0:T(8,128)} %copy-done.9, f32[5,8,128]{2,1,0:T(8,128)} %broadcast_in_dim.7.refs_1_, f32[16,128]{1,0:T(8,128)} %broadcast_in_dim.6.refs_1_.refs_2_, f32[256,256]{1,0:T(8,128)} %bitcast.82, ...), custom_call_target="tpu_custom_call" | custom-call | tf_op jit(solution)/shard_map/start/pallas_call | solution.py:83
  30.8 3.4 %all-to-all-start.1 = ((f32[8,10,8,128]{3,2,1,0:T(8,128)}), f32[8,10,8,128]{3,2,1,0:T(8,128)S(1)}, u32[]{:S(2)}, u32[]{:S(2)}) async-start(f32[8,10,8,128]{3,2,1,0:T(8,128)} %bitcast.87), calls=%async_computation.1 | async-start | bytes 655360 | tf_op jit(solution)/shard_map/all_to_all | solution.py:572
  35.1 7.6 %hidden.8 = (f32[20,16,128]{2,1,0:T(8,128)}, f32[8,128]{1,0:T(8,128)}, f32[10,256,512]{2,1,0:T(8,128)}, f32[10,256,512]{2,1,0:T(8,128)}) custom-call(s32[20]{0:T(128)} %bitcast.89, f32[56,128]{1,0:T(8,128)} %get-tuple-element.95.refs_1_.refs_2_, f32[256,256]{1,0:T(8,128)} %get-tuple-element.96.refs_2_.refs_3_, f32[8,128]{1,0:T(8,128)} %broadcast_in_dim.8.refs_3_, ...), custom_call_target="tpu_custom_call" | custom-call | flops 2013265920 | bytes 20971520 | tf_op jit(solution)/shard_map/hidden/pallas_call | solution.py:83
  42.8 2.3 all-to-all-done.1.recv_ref
  45.1 0.8 piece.4
  45.9 3.6 %all-to-all-start.2 = ((f32[8,10,8,128]{3,2,1,0:T(8,128)}), f32[8,10,8,128]{3,2,1,0:T(8,128)S(1)}, u32[]{:S(2)}, u32[]{:S(2)}) async-start(f32[8,10,8,128]{3,2,1,0:T(8,128)} %piece.4), calls=%async_computation.2 | async-start | bytes 655360 | tf_op jit(solution)/shard_map/all_to_all | solution.py:601
  50.0 7.5 %hidden.9 = (f32[20,16,128]{2,1,0:T(8,128)}, f32[8,128]{1,0:T(8,128)}, f32[10,256,512]{2,1,0:T(8,128)}, f32[10,256,512]{2,1,0:T(8,128)}) custom-call(s32[20]{0:T(128)} %bitcast.90, f32[56,128]{1,0:T(8,128)} %get-tuple-element.95.refs_1_.refs_2_, f32[256,256]{1,0:T(8,128)} %get-tuple-element.96.refs_2_.refs_3_, ...), custom_call_target="tpu_custom_call", output_to_operand_aliasing={{2}: (11, {}), {3}: (12, {})} | custom-call | flops 2013265920 | bytes 20971520 | tf_op jit(solution)/shard_map/hidden/pallas_call | solution.py:83
  58.2 2.0 all-to-all-done.2
  60.9 1.9 pack.4
  62.8 4.3 %all-to-all-start.3 = ((f32[32,1,128]{2,1,0:T(1,128)}), f32[32,1,128]{2,1,0:T(1,128)S(1)}, u32[]{:S(2)}, u32[]{:S(2)}) async-start(f32[32,1,128]{2,1,0:T(1,128)} %pack.4), calls=%async_computation.3 | async-start | bytes 32768 | tf_op jit(solution)/shard_map/all_to_all | solution.py:534
  67.1 0.7 maximum_select_fusion.refs_4_
  67.9 6.4 %all-to-all-done.3.refs_0_ = f32[32,1,128]{2,1,0:T(1,128)S(1)} async-done(((f32[32,1,128]{2,1,0:T(1,128)}), f32[32,1,128]{2,1,0:T(1,128)S(1)}, u32[]{:S(2)}, u32[]{:S(2)}) %all-to-all-start.3) | async-done | bytes 16416 | tf_op jit(solution)/shard_map/all_to_all | solution.py:534
  74.9 9.1 %update.4 = (f32[256,256]{1,0:T(8,128)}, f32[40,16,128]{2,1,0:T(8,128)}, f32[256,256]{1,0:T(8,128)}, f32[56,128]{1,0:T(8,128)}, f32[10,256,512]{2,1,0:T(8,128)}) custom-call(f32[32,1,128]{2,1,0:T(1,128)} %copy-done.15, f32[5,8,128]{2,1,0:T(8,128)} %broadcast_in_dim.7.refs_1_, f32[56,128]{1,0:T(8,128)} %get-tuple-element.95.refs_1_.refs_2_, ...), custom_call_target="tpu_custom_call" | custom-call | flops 10485760 | bytes 20971520 | tf_op jit(solution)/shard_map/update/pallas_call | solution.py:83
  84.0 3.4 %all-to-all-start.4 = ((f32[8,10,8,128]{3,2,1,0:T(8,128)}), f32[8,10,8,128]{3,2,1,0:T(8,128)S(1)}, u32[]{:S(2)}, u32[]{:S(2)}) async-start(f32[8,10,8,128]{3,2,1,0:T(8,128)} %bitcast.85), calls=%async_computation.4 | async-start | bytes 655360 | tf_op jit(solution)/shard_map/all_to_all | solution.py:572
  87.6 8.4 %hidden.10 = (f32[20,16,128]{2,1,0:T(8,128)}, f32[8,128]{1,0:T(8,128)}, f32[10,256,512]{2,1,0:T(8,128)}, f32[10,256,512]{2,1,0:T(8,128)}) custom-call(s32[20]{0:T(128)} %bitcast.91, f32[56,128]{1,0:T(8,128)} %get-tuple-element.116.refs_1_.refs_2_, f32[256,256]{1,0:T(8,128)} %get-tuple-element.117.refs_2_.refs_3_, f32[8,128]{1,0:T(8,128)} %broadcast_in_dim.8.refs_3_, ...), custom_call_target="tpu_custom_call" | custom-call | flops 2013265920 | bytes 20971520 | tf_op jit(solution)/shard_map/hidden/pallas_call | solution.py:83
  96.0 2.0 all-to-all-done.4.recv_ref
  98.0 0.8 piece.5
  98.8 3.9 %all-to-all-start.5 = ((f32[8,10,8,128]{3,2,1,0:T(8,128)}), f32[8,10,8,128]{3,2,1,0:T(8,128)S(1)}, u32[]{:S(2)}, u32[]{:S(2)}) async-start(f32[8,10,8,128]{3,2,1,0:T(8,128)} %piece.5), calls=%async_computation.5 | async-start | bytes 655360 | tf_op jit(solution)/shard_map/all_to_all | solution.py:601
  103.3 8.3 %hidden.11 = (f32[20,16,128]{2,1,0:T(8,128)}, f32[8,128]{1,0:T(8,128)}, f32[10,256,512]{2,1,0:T(8,128)}, f32[10,256,512]{2,1,0:T(8,128)}) custom-call(s32[20]{0:T(128)} %bitcast.92, f32[56,128]{1,0:T(8,128)} %get-tuple-element.116.refs_1_.refs_2_, f32[256,256]{1,0:T(8,128)} %get-tuple-element.117.refs_2_.refs_3_, ...), custom_call_target="tpu_custom_call", output_to_operand_aliasing={{2}: (12, {}), {3}: (13, {})} | custom-call | flops 2013265920 | bytes 20971520 | tf_op jit(solution)/shard_map/hidden/pallas_call | solution.py:83
  112.4 1.2 all-to-all-done.5
  114.3 1.9 pack.5
  116.2 4.9 %all-to-all-start.6 = ((f32[32,1,128]{2,1,0:T(1,128)}), f32[32,1,128]{2,1,0:T(1,128)S(1)}, u32[]{:S(2)}, u32[]{:S(2)}) async-start(f32[32,1,128]{2,1,0:T(1,128)} %pack.5), calls=%async_computation.6 | async-start | bytes 32768 | tf_op jit(solution)/shard_map/all_to_all | solution.py:534
  121.9 6.4 %all-to-all-done.6.refs_0_ = f32[32,1,128]{2,1,0:T(1,128)S(1)} async-done(((f32[32,1,128]{2,1,0:T(1,128)}), f32[32,1,128]{2,1,0:T(1,128)S(1)}, u32[]{:S(2)}, u32[]{:S(2)}) %all-to-all-start.6) | async-done | bytes 16416 | tf_op jit(solution)/shard_map/all_to_all | solution.py:534
  128.9 9.1 %update.5 = (f32[256,256]{1,0:T(8,128)}, f32[40,16,128]{2,1,0:T(8,128)}, f32[256,256]{1,0:T(8,128)}, f32[56,128]{1,0:T(8,128)}, f32[10,256,512]{2,1,0:T(8,128)}) custom-call(f32[32,1,128]{2,1,0:T(1,128)} %copy-done.16, f32[5,8,128]{2,1,0:T(8,128)} %broadcast_in_dim.7.refs_1_, f32[56,128]{1,0:T(8,128)} %get-tuple-element.116.refs_1_.refs_2_, ...), custom_call_target="tpu_custom_call" | custom-call | flops 10485760 | bytes 20971520 | tf_op jit(solution)/shard_map/update/pallas_call | solution.py:83
  138.0 3.4 %all-to-all-start.7 = ((f32[8,10,8,128]{3,2,1,0:T(8,128)}), f32[8,10,8,128]{3,2,1,0:T(8,128)S(1)}, u32[]{:S(2)}, u32[]{:S(2)}) async-start(f32[8,10,8,128]{3,2,1,0:T(8,128)} %bitcast.86), calls=%async_computation.7 | async-start | bytes 655360 | tf_op jit(solution)/shard_map/all_to_all | solution.py:572
  141.6 9.4 %hidden.12 = (f32[20,16,128]{2,1,0:T(8,128)}, f32[8,128]{1,0:T(8,128)}, f32[10,256,512]{2,1,0:T(8,128)}, f32[10,256,512]{2,1,0:T(8,128)}) custom-call(s32[20]{0:T(128)} %bitcast.93, f32[56,128]{1,0:T(8,128)} %get-tuple-element.137.refs_1_.refs_2_, f32[256,256]{1,0:T(8,128)} %get-tuple-element.138.refs_2_.refs_3_, f32[8,128]{1,0:T(8,128)} %broadcast_in_dim.8.refs_3_, ...), custom_call_target="tpu_custom_call" | custom-call | flops 2013265920 | bytes 20971520 | tf_op jit(solution)/shard_map/hidden/pallas_call | solution.py:83
  151.0 1.0 all-to-all-done.7.recv_ref
  152.0 0.8 piece.6
  152.7 4.8 %all-to-all-start.8 = ((f32[8,10,8,128]{3,2,1,0:T(8,128)}), f32[8,10,8,128]{3,2,1,0:T(8,128)S(1)}, u32[]{:S(2)}, u32[]{:S(2)}) async-start(f32[8,10,8,128]{3,2,1,0:T(8,128)} %piece.6), calls=%async_computation.8 | async-start | bytes 655360 | tf_op jit(solution)/shard_map/all_to_all | solution.py:601
  158.2 9.2 %hidden.13 = (f32[20,16,128]{2,1,0:T(8,128)}, f32[8,128]{1,0:T(8,128)}, f32[10,256,512]{2,1,0:T(8,128)}, f32[10,256,512]{2,1,0:T(8,128)}) custom-call(s32[20]{0:T(128)} %bitcast.94, f32[56,128]{1,0:T(8,128)} %get-tuple-element.137.refs_1_.refs_2_, f32[256,256]{1,0:T(8,128)} %get-tuple-element.138.refs_2_.refs_3_, ...), custom_call_target="tpu_custom_call", output_to_operand_aliasing={{2}: (13, {}), {3}: (14, {})} | custom-call | flops 2013265920 | bytes 20971520 | tf_op jit(solution)/shard_map/hidden/pallas_call | solution.py:83
  169.2 1.9 pack.6
  171.2 5.8 %all-to-all-start.9 = ((f32[32,1,128]{2,1,0:T(1,128)}), f32[32,1,128]{2,1,0:T(1,128)S(1)}, u32[]{:S(2)}, u32[]{:S(2)}) async-start(f32[32,1,128]{2,1,0:T(1,128)} %pack.6), calls=%async_computation.9 | async-start | bytes 32768 | tf_op jit(solution)/shard_map/all_to_all | solution.py:534
  177.7 6.4 %all-to-all-done.9.refs_0_ = f32[32,1,128]{2,1,0:T(1,128)S(1)} async-done(((f32[32,1,128]{2,1,0:T(1,128)}), f32[32,1,128]{2,1,0:T(1,128)S(1)}, u32[]{:S(2)}, u32[]{:S(2)}) %all-to-all-start.9) | async-done | bytes 16416 | tf_op jit(solution)/shard_map/all_to_all | solution.py:534
  184.7 9.1 %update.6 = (f32[256,256]{1,0:T(8,128)}, f32[40,16,128]{2,1,0:T(8,128)}, f32[256,256]{1,0:T(8,128)}, f32[56,128]{1,0:T(8,128)}, f32[10,256,512]{2,1,0:T(8,128)}) custom-call(f32[32,1,128]{2,1,0:T(1,128)} %copy-done.17, f32[5,8,128]{2,1,0:T(8,128)} %broadcast_in_dim.7.refs_1_, f32[56,128]{1,0:T(8,128)} %get-tuple-element.137.refs_1_.refs_2_, ...), custom_call_target="tpu_custom_call" | custom-call | flops 10485760 | bytes 20971520 | tf_op jit(solution)/shard_map/update/pallas_call | solution.py:83
  193.9 3.4 %all-to-all-start.10 = ((f32[8,10,8,128]{3,2,1,0:T(8,128)}), f32[8,10,8,128]{3,2,1,0:T(8,128)S(1)}, u32[]{:S(2)}, u32[]{:S(2)}) async-start(f32[8,10,8,128]{3,2,1,0:T(8,128)} %bitcast.84), calls=%async_computation.10 | async-start | bytes 655360 | tf_op jit(solution)/shard_map/all_to_all | solution.py:572
  197.4 9.9 %hidden.14 = (f32[20,16,128]{2,1,0:T(8,128)}, f32[8,128]{1,0:T(8,128)}, f32[10,256,512]{2,1,0:T(8,128)}, f32[10,256,512]{2,1,0:T(8,128)}) custom-call(s32[20]{0:T(128)} %bitcast.95, f32[56,128]{1,0:T(8,128)} %get-tuple-element.158.refs_1_.refs_2_, f32[256,256]{1,0:T(8,128)} %get-tuple-element.159.refs_2_.refs_3_, f32[8,128]{1,0:T(8,128)} %broadcast_in_dim.8.refs_3_, ...), custom_call_target="tpu_custom_call" | custom-call | flops 2013265920 | bytes 20971520 | tf_op jit(solution)/shard_map/hidden/pallas_call | solution.py:83
  207.8 0.8 piece.7
  208.6 5.4 %all-to-all-start.11 = ((f32[8,10,8,128]{3,2,1,0:T(8,128)}), f32[8,10,8,128]{3,2,1,0:T(8,128)S(1)}, u32[]{:S(2)}, u32[]{:S(2)}) async-start(f32[8,10,8,128]{3,2,1,0:T(8,128)} %piece.7), calls=%async_computation.11 | async-start | bytes 655360 | tf_op jit(solution)/shard_map/all_to_all | solution.py:601
  214.6 9.8 %hidden.15 = (f32[20,16,128]{2,1,0:T(8,128)}, f32[8,128]{1,0:T(8,128)}, f32[10,256,512]{2,1,0:T(8,128)}, f32[10,256,512]{2,1,0:T(8,128)}) custom-call(s32[20]{0:T(128)} %bitcast.96, f32[56,128]{1,0:T(8,128)} %get-tuple-element.158.refs_1_.refs_2_, f32[256,256]{1,0:T(8,128)} %get-tuple-element.159.refs_2_.refs_3_, ...), custom_call_target="tpu_custom_call", output_to_operand_aliasing={{2}: (14, {}), {3}: (15, {})} | custom-call | flops 2013265920 | bytes 20971520 | tf_op jit(solution)/shard_map/hidden/pallas_call | solution.py:83
  225.1 0.7 copy-done.5
  225.8 1.9 pack.7
  227.8 6.1 %all-to-all-start.12 = ((f32[32,1,128]{2,1,0:T(1,128)}), f32[32,1,128]{2,1,0:T(1,128)S(1)}, u32[]{:S(2)}, u32[]{:S(2)}) async-start(f32[32,1,128]{2,1,0:T(1,128)} %pack.7), calls=%async_computation.12 | async-start | bytes 32768 | tf_op jit(solution)/shard_map/all_to_all | solution.py:534
  233.9 0.7 maximum_select_fusion.3.refs_4_
  234.7 6.4 %all-to-all-done.12.refs_0_ = f32[32,1,128]{2,1,0:T(1,128)S(1)} async-done(((f32[32,1,128]{2,1,0:T(1,128)}), f32[32,1,128]{2,1,0:T(1,128)S(1)}, u32[]{:S(2)}, u32[]{:S(2)}) %all-to-all-start.12) | async-done | bytes 16416 | tf_op jit(solution)/shard_map/all_to_all | solution.py:534
  241.6 8.9 %update.7 = (f32[256,256]{1,0:T(8,128)}, f32[16,5120]{1,0:T(8,128)}, f32[256,5120]{1,0:T(8,128)}) custom-call(f32[32,1,128]{2,1,0:T(1,128)} %copy-done.14, f32[5,8,128]{2,1,0:T(8,128)} %broadcast_in_dim.7.refs_1_, f32[56,128]{1,0:T(8,128)} %get-tuple-element.158.refs_1_.refs_2_, f32[256,256]{1,0:T(8,128)} %get-tuple-element.159.refs_2_.refs_3_, ...), custom_call_target="tpu_custom_call" | custom-call | flops 10485760 | bytes 20971520 | tf_op jit(solution)/shard_map/update/pallas_call | solution.py:83
  (82 shorter events, 15.1 us)
Async XLA Ops:
  0.6 14.1 %copy-start.18 = (s32[5]{0:T(128)S(1)}, s32[5]{0:T(128)}, u32[]{:S(2)}) copy-start(s32[5]{0:T(128)} %param.19) | copy-start | bytes 64
  0.6 14.1 %copy-start.19 = (s32[5]{0:T(128)S(1)}, s32[5]{0:T(128)}, u32[]{:S(2)}) copy-start(s32[5]{0:T(128)} %param.18) | copy-start | bytes 64
  7.4 15.5 %all-to-all-start = ((f32[32,8,128]{2,1,0:T(8,128)}), f32[32,8,128]{2,1,0:T(8,128)S(1)}, u32[]{:S(2)}, u32[]{:S(2)}) async-start(f32[32,8,128]{2,1,0:T(8,128)} %get-tuple-element.92), calls=%async_computation | async-start | bytes 262144 | tf_op jit(solution)/shard_map/all_to_all | solution.py:534
  22.9 0.6 copy-start.9
  30.8 14.3 %all-to-all-start.1 = ((f32[8,10,8,128]{3,2,1,0:T(8,128)}), f32[8,10,8,128]{3,2,1,0:T(8,128)S(1)}, u32[]{:S(2)}, u32[]{:S(2)}) async-start(f32[8,10,8,128]{3,2,1,0:T(8,128)} %bitcast.87), calls=%async_computation.1 | async-start | bytes 655360 | tf_op jit(solution)/shard_map/all_to_all | solution.py:572
  34.3 15.3 %collective-permute-start = (f32[256,256]{1,0:T(8,128)}, f32[256,256]{1,0:T(8,128)S(1)}, u32[]{:S(2)}, u32[]{:S(2)}) collective-permute-start(f32[256,256]{1,0:T(8,128)} %get-tuple-element.102), channel_id=1, source_target_pairs={{0,1},{1,0},{2,3},{3,2},{4,5},{5,4},{6,7},{7,6},{8,9},{9,8},{10,11... | collective-permute-start | bytes 786440 | tf_op jit(solution)/shard_map/ppermute | solution.py:573
  35.1 14.3 %copy-start.8 = (f32[16,16,256]{2,1,0:T(8,128)S(1)}, f32[16,16,256]{2,1,0:T(8,128)}, u32[]{:S(2)}) copy-start(f32[16,16,256]{2,1,0:T(8,128)} %param.10) | copy-start | bytes 786436
  35.1 14.4 %copy-start.10 = (f32[256,256]{1,0:T(8,128)S(1)}, f32[256,256]{1,0:T(8,128)}, u32[]{:S(2)}) copy-start(f32[256,256]{1,0:T(8,128)} %get-tuple-element.102) | copy-start | bytes 786436
  45.9 14.3 %all-to-all-start.2 = ((f32[8,10,8,128]{3,2,1,0:T(8,128)}), f32[8,10,8,128]{3,2,1,0:T(8,128)S(1)}, u32[]{:S(2)}, u32[]{:S(2)}) async-start(f32[8,10,8,128]{3,2,1,0:T(8,128)} %piece.4), calls=%async_computation.2 | async-start | bytes 655360 | tf_op jit(solution)/shard_map/all_to_all | solution.py:601
  49.6 7.9 %collective-permute-start.1 = (f32[128,256]{1,0:T(8,128)S(1)}, f32[128,256]{1,0:T(8,128)S(1)}, u32[]{:S(2)}, u32[]{:S(2)}) collective-permute-start(f32[128,256]{1,0:T(8,128)S(1)} %dynamic-slice_add_fusion.3.near_ref), channel_id=1, source_target_pairs={{0,2},{1,3},{2,0},{3,1},{4,6},{5,7},{6,4},{7,5},{8,10},{9,11},{10,... | collective-permute-start | bytes 393224 | tf_op jit(solution)/shard_map/ppermute | solution.py:610
  57.6 0.6 copy-start
  58.2 9.0 %collective-permute-start.2 = (f32[128,256]{1,0:T(8,128)S(1)}, f32[128,256]{1,0:T(8,128)S(1)}, u32[]{:S(2)}, u32[]{:S(2)}) collective-permute-start(f32[128,256]{1,0:T(8,128)S(1)} %get-tuple-element.112), channel_id=1, source_target_pairs={{0,1},{1,0},{2,3},{3,2},{4,5},{5,4},{6,7},{7,6},{8,9},{9,8},{10,11... | collective-permute-start | bytes 393224 | tf_op jit(solution)/shard_map/ppermute | solution.py:621
  60.2 0.7 copy-start.4
  62.8 11.5 %all-to-all-start.3 = ((f32[32,1,128]{2,1,0:T(1,128)}), f32[32,1,128]{2,1,0:T(1,128)S(1)}, u32[]{:S(2)}, u32[]{:S(2)}) async-start(f32[32,1,128]{2,1,0:T(1,128)} %pack.4), calls=%async_computation.3 | async-start | bytes 32768 | tf_op jit(solution)/shard_map/all_to_all | solution.py:534
  74.3 0.6 copy-start.15
  84.0 14.0 %all-to-all-start.4 = ((f32[8,10,8,128]{3,2,1,0:T(8,128)}), f32[8,10,8,128]{3,2,1,0:T(8,128)S(1)}, u32[]{:S(2)}, u32[]{:S(2)}) async-start(f32[8,10,8,128]{3,2,1,0:T(8,128)} %bitcast.85), calls=%async_computation.4 | async-start | bytes 655360 | tf_op jit(solution)/shard_map/all_to_all | solution.py:572
  87.5 15.2 %collective-permute-start.3 = (f32[256,256]{1,0:T(8,128)}, f32[256,256]{1,0:T(8,128)S(1)}, u32[]{:S(2)}, u32[]{:S(2)}) collective-permute-start(f32[256,256]{1,0:T(8,128)} %get-tuple-element.123), channel_id=1, source_target_pairs={{0,1},{1,0},{2,3},{3,2},{4,5},{5,4},{6,7},{7,6},{8,9},{9,8},{10,11... | collective-permute-start | bytes 786440 | tf_op jit(solution)/shard_map/ppermute | solution.py:573
  87.6 15.1 %copy-start.12 = (f32[256,256]{1,0:T(8,128)S(1)}, f32[256,256]{1,0:T(8,128)}, u32[]{:S(2)}) copy-start(f32[256,256]{1,0:T(8,128)} %get-tuple-element.123) | copy-start | bytes 786436
  98.8 14.8 %all-to-all-start.5 = ((f32[8,10,8,128]{3,2,1,0:T(8,128)}), f32[8,10,8,128]{3,2,1,0:T(8,128)S(1)}, u32[]{:S(2)}, u32[]{:S(2)}) async-start(f32[8,10,8,128]{3,2,1,0:T(8,128)} %piece.5), calls=%async_computation.5 | async-start | bytes 655360 | tf_op jit(solution)/shard_map/all_to_all | solution.py:601
  102.7 9.0 %collective-permute-start.4 = (f32[128,256]{1,0:T(8,128)S(1)}, f32[128,256]{1,0:T(8,128)S(1)}, u32[]{:S(2)}, u32[]{:S(2)}) collective-permute-start(f32[128,256]{1,0:T(8,128)S(1)} %dynamic-slice_add_fusion.2.near_ref), channel_id=1, source_target_pairs={{0,2},{1,3},{2,0},{3,1},{4,6},{5,7},{6,4},{7,5},{8,10},{9,11},{10,... | collective-permute-start | bytes 393224 | tf_op jit(solution)/shard_map/ppermute | solution.py:610
  111.8 0.6 copy-start.2
  112.4 8.8 %collective-permute-start.5 = (f32[128,256]{1,0:T(8,128)S(1)}, f32[128,256]{1,0:T(8,128)S(1)}, u32[]{:S(2)}, u32[]{:S(2)}) collective-permute-start(f32[128,256]{1,0:T(8,128)S(1)} %get-tuple-element.133), channel_id=1, source_target_pairs={{0,1},{1,0},{2,3},{3,2},{4,5},{5,4},{6,7},{7,6},{8,9},{9,8},{10,11... | collective-permute-start | bytes 393224 | tf_op jit(solution)/shard_map/ppermute | solution.py:621
  113.6 0.7 copy-start.6
  116.2 12.1 %all-to-all-start.6 = ((f32[32,1,128]{2,1,0:T(1,128)}), f32[32,1,128]{2,1,0:T(1,128)S(1)}, u32[]{:S(2)}, u32[]{:S(2)}) async-start(f32[32,1,128]{2,1,0:T(1,128)} %pack.5), calls=%async_computation.6 | async-start | bytes 32768 | tf_op jit(solution)/shard_map/all_to_all | solution.py:534
  128.3 0.6 copy-start.16
  138.0 14.0 %all-to-all-start.7 = ((f32[8,10,8,128]{3,2,1,0:T(8,128)}), f32[8,10,8,128]{3,2,1,0:T(8,128)S(1)}, u32[]{:S(2)}, u32[]{:S(2)}) async-start(f32[8,10,8,128]{3,2,1,0:T(8,128)} %bitcast.86), calls=%async_computation.7 | async-start | bytes 655360 | tf_op jit(solution)/shard_map/all_to_all | solution.py:572
  141.5 16.1 %collective-permute-start.6 = (f32[256,256]{1,0:T(8,128)}, f32[256,256]{1,0:T(8,128)S(1)}, u32[]{:S(2)}, u32[]{:S(2)}) collective-permute-start(f32[256,256]{1,0:T(8,128)} %get-tuple-element.144), channel_id=1, source_target_pairs={{0,1},{1,0},{2,3},{3,2},{4,5},{5,4},{6,7},{7,6},{8,9},{9,8},{10,11... | collective-permute-start | bytes 786440 | tf_op jit(solution)/shard_map/ppermute | solution.py:573
  141.6 16.0 %copy-start.13 = (f32[256,256]{1,0:T(8,128)S(1)}, f32[256,256]{1,0:T(8,128)}, u32[]{:S(2)}) copy-start(f32[256,256]{1,0:T(8,128)} %get-tuple-element.144) | copy-start | bytes 786436
  152.7 15.8 %all-to-all-start.8 = ((f32[8,10,8,128]{3,2,1,0:T(8,128)}), f32[8,10,8,128]{3,2,1,0:T(8,128)S(1)}, u32[]{:S(2)}, u32[]{:S(2)}) async-start(f32[8,10,8,128]{3,2,1,0:T(8,128)} %piece.6), calls=%async_computation.8 | async-start | bytes 655360 | tf_op jit(solution)/shard_map/all_to_all | solution.py:601
  157.6 9.9 %collective-permute-start.7 = (f32[128,256]{1,0:T(8,128)S(1)}, f32[128,256]{1,0:T(8,128)S(1)}, u32[]{:S(2)}, u32[]{:S(2)}) collective-permute-start(f32[128,256]{1,0:T(8,128)S(1)} %dynamic-slice_add_fusion.1.near_ref), channel_id=1, source_target_pairs={{0,2},{1,3},{2,0},{3,1},{4,6},{5,7},{6,4},{7,5},{8,10},{9,11},{10,... | collective-permute-start | bytes 393224 | tf_op jit(solution)/shard_map/ppermute | solution.py:610
  167.6 0.6 copy-start.3
  168.2 8.8 %collective-permute-start.8 = (f32[128,256]{1,0:T(8,128)S(1)}, f32[128,256]{1,0:T(8,128)S(1)}, u32[]{:S(2)}, u32[]{:S(2)}) collective-permute-start(f32[128,256]{1,0:T(8,128)S(1)} %get-tuple-element.154), channel_id=1, source_target_pairs={{0,1},{1,0},{2,3},{3,2},{4,5},{5,4},{6,7},{7,6},{8,9},{9,8},{10,11... | collective-permute-start | bytes 393224 | tf_op jit(solution)/shard_map/ppermute | solution.py:621
  168.5 0.7 copy-start.7
  171.2 13.0 %all-to-all-start.9 = ((f32[32,1,128]{2,1,0:T(1,128)}), f32[32,1,128]{2,1,0:T(1,128)S(1)}, u32[]{:S(2)}, u32[]{:S(2)}) async-start(f32[32,1,128]{2,1,0:T(1,128)} %pack.6), calls=%async_computation.9 | async-start | bytes 32768 | tf_op jit(solution)/shard_map/all_to_all | solution.py:534
  184.1 0.6 copy-start.17
  193.9 14.0 %all-to-all-start.10 = ((f32[8,10,8,128]{3,2,1,0:T(8,128)}), f32[8,10,8,128]{3,2,1,0:T(8,128)S(1)}, u32[]{:S(2)}, u32[]{:S(2)}) async-start(f32[8,10,8,128]{3,2,1,0:T(8,128)} %bitcast.84), calls=%async_computation.10 | async-start | bytes 655360 | tf_op jit(solution)/shard_map/all_to_all | solution.py:572
  197.3 16.6 %collective-permute-start.9 = (f32[256,256]{1,0:T(8,128)}, f32[256,256]{1,0:T(8,128)S(1)}, u32[]{:S(2)}, u32[]{:S(2)}) collective-permute-start(f32[256,256]{1,0:T(8,128)} %get-tuple-element.165), channel_id=1, source_target_pairs={{0,1},{1,0},{2,3},{3,2},{4,5},{5,4},{6,7},{7,6},{8,9},{9,8},{10,11... | collective-permute-start | bytes 786440 | tf_op jit(solution)/shard_map/ppermute | solution.py:573
  197.4 16.6 %copy-start.11 = (f32[256,256]{1,0:T(8,128)S(1)}, f32[256,256]{1,0:T(8,128)}, u32[]{:S(2)}) copy-start(f32[256,256]{1,0:T(8,128)} %get-tuple-element.165) | copy-start | bytes 786436
  208.6 16.5 %all-to-all-start.11 = ((f32[8,10,8,128]{3,2,1,0:T(8,128)}), f32[8,10,8,128]{3,2,1,0:T(8,128)S(1)}, u32[]{:S(2)}, u32[]{:S(2)}) async-start(f32[8,10,8,128]{3,2,1,0:T(8,128)} %piece.7), calls=%async_computation.11 | async-start | bytes 655360 | tf_op jit(solution)/shard_map/all_to_all | solution.py:601
  214.0 10.4 %collective-permute-start.10 = (f32[128,256]{1,0:T(8,128)S(1)}, f32[128,256]{1,0:T(8,128)S(1)}, u32[]{:S(2)}, u32[]{:S(2)}) collective-permute-start(f32[128,256]{1,0:T(8,128)S(1)} %dynamic-slice_add_fusion.near_ref), channel_id=1, source_target_pairs={{0,2},{1,3},{2,0},{3,1},{4,6},{5,7},{6,4},{7,5},{8,10},{9,11},{10,... | collective-permute-start | bytes 393224 | tf_op jit(solution)/shard_map/ppermute | solution.py:610
  224.5 0.6 copy-start.1
  225.1 8.8 %collective-permute-start.11 = (f32[128,256]{1,0:T(8,128)S(1)}, f32[128,256]{1,0:T(8,128)S(1)}, u32[]{:S(2)}, u32[]{:S(2)}) collective-permute-start(f32[128,256]{1,0:T(8,128)S(1)} %get-tuple-element.175), channel_id=1, source_target_pairs={{0,1},{1,0},{2,3},{3,2},{4,5},{5,4},{6,7},{7,6},{8,9},{9,8},{10,11... | collective-permute-start | bytes 393224 | tf_op jit(solution)/shard_map/ppermute | solution.py:621
  225.1 0.7 copy-start.5
  227.8 13.2 %all-to-all-start.12 = ((f32[32,1,128]{2,1,0:T(1,128)}), f32[32,1,128]{2,1,0:T(1,128)S(1)}, u32[]{:S(2)}, u32[]{:S(2)}) async-start(f32[32,1,128]{2,1,0:T(1,128)} %pack.7), calls=%async_computation.12 | async-start | bytes 32768 | tf_op jit(solution)/shard_map/all_to_all | solution.py:534
  241.0 0.6 copy-start.14

commit v2 on v1

--- a/solution.py
+++ b/solution.py
@@ -41,7 +41,7 @@
     return jnp.sum(jnp.sum(x, axis=1, keepdims=True), axis=0, keepdims=True)
 
 
-def stage(body, n_small, n_large, n_small_out, n_large_out, extra):
+def stage(body, n_near, n_small, n_large, n_small_out, n_large_out, extra):
     def kernel(*refs):
         refs = list(refs)
 
@@ -50,7 +50,7 @@
             del refs[:n]
             return out
 
-        first, small, large = take(extra), take(n_small), take(n_large)
+        first, near, small, large = take(extra), take(n_near), take(n_small), take(n_large)
         small_out, large_out = take(n_small_out), take(n_large_out)
         held, made = take(n_small), take(n_small_out)
         in_sems, out_sems = take(2)
@@ -62,7 +62,7 @@
             for copy in loads:
                 copy.wait()
 
-        finish = body(ready, first, held, large, made, large_out, refs)
+        finish = body(ready, first, near + held, large, made, large_out, refs)
         stores = [pltpu.make_async_copy(b, a, out_sems.at[j]) for j, (a, b) in enumerate(zip(small_out, made))]
         for copy in stores:
             copy.start()
@@ -73,35 +73,50 @@
     return kernel
 
 
+def far_away(x):
+    return pltpu.with_memory_space_constraint(x, pltpu.HBM)
+
+
 def staged_call(
-    body, first, small, large, small_out, large_out, scratch, name, cost=None, aliases=None
+    body, first, near, small, large, small_out, large_out, scratch, name, cost=None, aliases=None,
+    limit=48,
 ):
     dma = pltpu.SemaphoreType.DMA
     hbm = pl.BlockSpec(memory_space=pl.ANY)
-    begin = len(first) + len(small)
+    begin = len(first) + len(near) + len(small)
+    held = [pltpu.VMEM(v.shape, v.dtype) for v in small + small_out]
     alias = {begin + a: len(small_out) + b for a, b in (aliases or {}).items()}
     return pl.pallas_call(
-        stage(body, len(small), len(large), len(small_out), len(large_out), len(first)),
-        in_specs=[pl.BlockSpec(memory_space=pltpu.SMEM)] * len(first) + [hbm] * (len(small) + len(large)),
+        stage(body, len(near), len(small), len(large), len(small_out), len(large_out), len(first)),
+        in_specs=[pl.BlockSpec(memory_space=pltpu.SMEM)] * len(first)
+        + [pl.BlockSpec(memory_space=pltpu.VMEM)] * len(near)
+        + [hbm] * (len(small) + len(large)),
         out_specs=[hbm] * (len(small_out) + len(large_out)),
-        out_shape=small_out + large_out,
-        scratch_shapes=[pltpu.VMEM(v.shape, v.dtype) for v in small + small_out]
+        out_shape=small_out + [pltpu.HBM(v.shape, v.dtype) for v in large_out],
+        scratch_shapes=held
         + [dma((max(1, len(small)),)), dma((max(1, len(small_out)),))]
         + scratch,
         input_output_aliases=alias,
-        compiler_params=params(60),
+        compiler_params=params(limit),
         cost_estimate=cost,
         name=name,
-    )(*first, *small, *large)
+    )(*first, *near, *small, *[far_away(v) for v in large])
 
 
 def lanes(c, width, t=0, size=None):
     return pl.ds(pl.multiple_of(c * width + t, LANES), width if size is None else size)
 
 
+def scen_levels(dims):
+    ids = lax.broadcasted_iota(jnp.int32, (dims.local_scen, 1), 0)
+    ids = ids + lax.axis_index("scen") * dims.local_scen
+    return 0.2 + 0.6 * (ids.astype(F32) + 0.5) / dims.total_scen
+
+
 def first_body(dims, ready, first, small, large, made, large_out, scratch):
     (mask_ref,) = first
-    level_ref, load_ref, lin_ref, diag_ref, cap_ref, zone_ref = small
+    load_ref, lin_ref, diag_ref, cap_ref, zone_ref = small
+    level = scen_levels(dims)
     cost_in, coup_in = large
     base_ref, pack_ref = made
     sums, capz, cost, coup, sems = scratch
@@ -128,13 +143,13 @@
     for s in range(ns):
         part = load_ref[s * periods : (s + 1) * periods, :]
         load += part * part
-        weighted += level_ref[s : s + 1, 0:1] * part
+        weighted += level[s : s + 1] * part
 
     @pl.loop(0, chunks)
     def _(c):
         for copy in copies(c):
             copy.wait()
-        levels = level_ref[:, 0:1]
+        levels = scen_levels(dims)
         dual = jnp.zeros((1, tile), F32)
         caps = jnp.zeros((1, tile), F32)
         for t in range(per):
@@ -149,6 +164,7 @@
                 (diag_ref[:, cols] + PENALTY) * dispatch + products - PENALTY * dims.mean_level * cap
             )
             base_ref[:, cols] = base
+
             dual += (
                 periods * jnp.sum(base * base, axis=0, keepdims=True)
                 + 2.0
@@ -208,10 +224,11 @@
 
 
 def start_body(dims, ready, first, small, large, made, large_out, scratch):
-    recv_ref, size_ref, level_ref, load_ref, base_ref, lin_ref, diag_ref, cap_ref, zone_ref = small
+    recv_ref, size_ref, load_ref, base_ref, lin_ref, diag_ref, cap_ref, zone_ref = small
     col_ref, price_ref, tot_ref, coef_ref = made
     (disp_ref,) = large_out
     buf, sems = scratch
+    level = scen_levels(dims)
     ns, periods = dims.local_scen, dims.periods
     zones = load_ref.shape[1]
     chunks, width = buf.shape[0], buf.shape[2]
@@ -227,7 +244,7 @@
     keep(coef_ref, None, 0, move, shift, size)
     for s in range(ns):
         rows = slice(s * periods, (s + 1) * periods)
-        price_ref[rows, :] = price * (level_ref[s : s + 1, 0:1] * scaled - load_ref[rows, :])
+        price_ref[rows, :] = price * (level[s : s + 1] * scaled - load_ref[rows, :])
     tot_ref[...] = jnp.zeros_like(tot_ref)
 
     @pl.loop(0, chunks)
@@ -239,7 +256,7 @@
             cap, stiff, lin = cap_ref[:, here], diag_ref[:, here] + PENALTY, lin_ref[:, here]
             lowest, highest = 0.02 * cap, 0.98 * cap
             acc = jnp.zeros((periods, LANES), F32)
-            dispatch = level_ref[:, 0:1] * cap
+            dispatch = scen_levels(dims) * cap
             weight = move / (stiff + 1.0 / dispatch + 1.0 / (cap - dispatch))
             base = base_ref[:, here]
             for s in range(ns):
@@ -261,7 +278,7 @@
 
 
 def update_body(dims, k, last, ready, first, small, large, made, large_out, scratch):
-    recv_ref, size_ref, coef_in, price_in, imb_ref, plan_ref, cap_ref, zone_ref = small
+    recv_ref, imb_ref, size_ref, coef_in, price_in, plan_ref, cap_ref, zone_ref = small
     if last:
         price_ref, plan_out = made
     else:
@@ -443,7 +460,7 @@
 
 
 def pack_body(dims, ready, first, small, large, made, large_out, scratch):
-    plan_ref, part_ref, primal_ref = small[:3]
+    plan_ref, primal_ref, part_ref = small[:3]
     (out_ref,) = made
     ready()
     cross = jnp.zeros(plan_ref.shape[1:], F32)
@@ -507,9 +524,6 @@
     mask = block_map.reshape(blocks)
     sizes = step_numer.astype(F32) / step_denom.astype(F32)
     sizes = lax.optimization_barrier(jnp.broadcast_to(sizes[:, None, None], (iters, 8, LANES)))
-    scen_ids = lax.axis_index("scen") * local_scen + jnp.arange(local_scen, dtype=jnp.int32)
-    levels = 0.2 + 0.6 * (scen_ids.astype(F32) + 0.5) / total_scen
-    levels = jnp.broadcast_to(levels[:, None], (local_scen, LANES))
 
     shape = jax.ShapeDtypeStruct
     dma = pltpu.SemaphoreType.DMA
@@ -536,18 +550,18 @@
     pack_rows = -(-(1 + 2 * (zones // LANES)) // 8) * 8
     tiles = pltpu.VMEM((chunks, per, tile, tile), BF16)
     base, packed = staged_call(
-        functools.partial(first_body, dims), [mask], [levels, load] + vector, [cost_c, coup_c],
+        functools.partial(first_body, dims), [mask], [], [load] + vector, [cost_c, coup_c],
         [shape((local_scen, local_gen), F32), shape((devices, pack_rows, LANES), F32)], [],
         [
             pltpu.VMEM((8, tile), F32), pltpu.VMEM((24, zones), F32), tiles, tiles,
             dma((2, chunks)),
         ],
-        "first",
+        "first", limit=60,
     )
     recv = exchange(packed)
 
     col_sums, prices, totals, coef, dispatch = staged_call(
-        functools.partial(start_body, dims), [], [recv, sizes, levels, load, base] + vector, [],
+        functools.partial(start_body, dims), [], [recv], [sizes, load, base] + vector, [],
         [col_shape, grid_shape, grid_shape, coef_shape], [state], [buffer, dma((chunks,))],
         "start",
     )
@@ -581,7 +595,7 @@
             carry = [resid, weight] if part else []
             col_k, partial, resid, weight = staged_call(
                 functools.partial(hidden_body, dims, k, last, begin, count),
-                [mask], [coef, prices, partial] + vector, [*past, cost_c, coup_c, *carry],
+                [mask], [], [coef, prices, partial] + vector, [*past, cost_c, coup_c, *carry],
                 [shape((count * width // LANES, periods, LANES), F32), part_shape], [state, state],
                 [
                     pltpu.VMEM((rows, zones), BF16), pltpu.VMEM((rows, zones), BF16),
@@ -624,24 +638,24 @@
         )
 
         (packed,) = staged_call(
-            functools.partial(pack_body, dims), [], [plan, partial, primal, *cols], [],
-            [shape((devices, 1, LANES), F32)], [], [], "pack",
+            functools.partial(pack_body, dims), [], [plan, primal, partial], [far_away(v) for v in cols], [],
+            [shape((devices, 1, LANES), F32)], [], [], "pack", limit=4,
         )
         recv = exchange(packed)
 
-        small = [recv, sizes, coef, prices, imbalance, plan, cap, zone]
+        near, small = [recv], [imbalance, sizes, coef, prices, plan, cap, zone]
         large = [dispatch, resid, weight]
         scratch = [buffer] * 3 + [pltpu.VMEM((8, LANES), F32), dma((3, chunks)), dma((chunks,))]
         cost = estimate(rows * local_gen * 8, rows * local_gen * 16)
         body = functools.partial(update_body, dims, k, last)
         if last:
             prices, plan, dispatch = staged_call(
-                body, [], small, large, [grid_shape, plan_shape], [shape((rows, local_gen), F32)],
+                body, [], near, small, large, [grid_shape, plan_shape], [shape((rows, local_gen), F32)],
                 scratch, "update", cost,
             )
         else:
             prices, col_sums, totals, coef, dispatch = staged_call(
-                body, [], small, large, [grid_shape, col_shape, grid_shape, coef_shape], [state],
+                body, [], near, small, large, [grid_shape, col_shape, grid_shape, coef_shape], [state],
                 scratch, "update", cost,
             )
             past.append(dispatch)

time: 252 us -> 242 us (0.960)
  local copies, waits for them, and re-layouts: 10.2 us -> 3.89 us
  waiting for transfers between devices: 42.5 us -> 46.8 us
  Pallas kernels: 131 us -> 127 us
  other arithmetic: 3.04 us -> 0.2 us
    unnamed x40 -> x34, local copies, waits for them, and re-layouts: 8.29 us -> 3.81 us
    pallas_call x18, Pallas kernels: 127 us -> 124 us  [staged_call(): pl.pallas_call(stage(body, len(near), len(small), len(large), len(small_o...]
    all_to_all x5, waiting for transfers between devices: 33.2 us -> 36.3 us  [exchange(): return lax.all_to_all(x, ('scen', 'gen'), 0, 0)]
    select_n x4, other arithmetic: 2.93 us -> 0.09 us  [local(): jnp.where(odd == 0, jnp.concatenate([mine, other]), jnp.concatenate([othe...]
  transfers between devices with their start and end apart: 25 -> 25, of which waited for: 12 -> 12; matrix products, arithmetic and copies ran while one was open for 2% -> 0% of each run, Pallas kernels for 32% -> 33%
where the time goes in v2:
time: 242 us; the launch traced here: 241 us
  Pallas kernels  127 us (52%)
  starting transfers between devices  61.9 us (26%)
  waiting for transfers between devices  46.8 us (19%)
  local copies, waits for them, and re-layouts  3.89 us (2%)
    pallas_call x18, Pallas kernels, staged_call(): pl.pallas_call(stage(body, len(near), len(small), len(large), len(small_o...  124 us
    all_to_all x5, waiting for transfers between devices, exchange(): return lax.all_to_all(x, ('scen', 'gen'), 0, 0)  36.3 us
    all_to_all x5, starting transfers between devices, exchange(): return lax.all_to_all(x, ('scen', 'gen'), 0, 0)  28.2 us
    all_to_all x4, starting transfers between devices, local(): gathered = lax.all_to_all(piece, 'scen', 0, 0)  17.2 us
    all_to_all x4, starting transfers between devices, local(): got = lax.all_to_all(flat, 'scen', 0, 0)  13.8 us
    all_to_all x4, waiting for transfers between devices, local(): got = lax.all_to_all(flat, 'scen', 0, 0)  6.58 us
  transfers between devices with their start and end apart: 25, of which 12 were waited for; matrix products, arithmetic and copies ran while one was open for 0% of the time, Pallas kernels for 33%

profile of v2, /device:TPU:0, one launch (start us, length us, event | category | flops | bytes accessed | tf_op | source)
XLA Modules:
  0.0 241.2 jit_solution(12108493267046702999)
XLA Ops:
  0.7 5.9 %first.1 = (f32[16,5120]{1,0:T(8,128)}, f32[32,8,128]{2,1,0:T(8,128)}) custom-call(s32[20]{0:T(128)} %bitcast.66, f32[256,256]{1,0:T(8,128)} %bitcast.63, f32[16,5120]{1,0:T(8,128)} %refs_4_.17, f32[1,5120]{1,0:T(1,128)} %bitcast.53, f32[1,5120]{1,0:T(1,128)} %bitcast.17, s32[1,5120]{1,0:T(1,128)} %bitcast.31, bf16[10,2,256,256]{3,2,1,0:T(8,128)(2,1)} %bitcast.75, ...), custom_call_target="tpu_custom_call" | custom-call | tf_op jit(solution)/shard_map/first/pallas_call | solution.py:89
  6.6 7.3 %all-to-all-start = ((f32[32,8,128]{2,1,0:T(8,128)}), f32[32,8,128]{2,1,0:T(8,128)S(1)}, u32[]{:S(2)}, u32[]{:S(2)}) async-start(f32[32,8,128]{2,1,0:T(8,128)} %get-tuple-element.92), calls=%async_computation | async-start | bytes 262144 | tf_op jit(solution)/shard_map/all_to_all | solution.py:548
  14.0 8.1 %all-to-all-done.refs_0_ = f32[32,8,128]{2,1,0:T(8,128)S(1)} async-done(((f32[32,8,128]{2,1,0:T(8,128)}), f32[32,8,128]{2,1,0:T(8,128)S(1)}, u32[]{:S(2)}, u32[]{:S(2)}) %all-to-all-start) | async-done | bytes 131104 | tf_op jit(solution)/shard_map/all_to_all | solution.py:548
  22.2 1.0 copy-done.5
  23.2 6.2 %start.1 = (f32[40,16,128]{2,1,0:T(8,128)}, f32[256,256]{1,0:T(8,128)S(1)}, f32[256,256]{1,0:T(8,128)S(1)}, f32[56,128]{1,0:T(8,128)S(1)}, f32[10,256,512]{2,1,0:T(8,128)}) custom-call(f32[32,8,128]{2,1,0:T(8,128)S(1)} %all-to-all-done.refs_0_, f32[5,8,128]{2,1,0:T(8,128)S(1)} %broadcast_in_dim.4.refs_1_.refs_2_, f32[256,256]{1,0:T(8,128)S(1)} %bitcast.64, ...), custom_call_target="tpu_custom_call" | custom-call | tf_op jit(solution)/shard_map/start/pallas_call | solution.py:89
  29.3 3.4 %all-to-all-start.1 = ((f32[8,10,8,128]{3,2,1,0:T(8,128)}), f32[8,10,8,128]{3,2,1,0:T(8,128)S(1)}, u32[]{:S(2)}, u32[]{:S(2)}) async-start(f32[8,10,8,128]{3,2,1,0:T(8,128)} %bitcast.7), calls=%async_computation.1 | async-start | bytes 655360 | tf_op jit(solution)/shard_map/all_to_all | solution.py:586
  33.1 7.4 %hidden.8 = (f32[20,16,128]{2,1,0:T(8,128)S(1)}, f32[8,128]{1,0:T(8,128)S(1)}, f32[10,256,512]{2,1,0:T(8,128)}, f32[10,256,512]{2,1,0:T(8,128)}) custom-call(s32[20]{0:T(128)S(1)} %bitcast.67, f32[56,128]{1,0:T(8,128)S(1)} %get-tuple-element.95.refs_1_.refs_3_, f32[256,256]{1,0:T(8,128)S(1)} %get-tuple-element.96.refs_2_.refs_4_, ...), custom_call_target="tpu_custom_call" | custom-call | flops 2013265920 | bytes 20971520 | tf_op jit(solution)/shard_map/hidden/pallas_call | solution.py:89
  40.4 0.7 copy-done.6
  41.1 2.5 %all-to-all-done.1.recv_ref = f32[8,10,8,128]{3,2,1,0:T(8,128)S(1)} async-done(((f32[8,10,8,128]{3,2,1,0:T(8,128)}), f32[8,10,8,128]{3,2,1,0:T(8,128)S(1)}, u32[]{:S(2)}, u32[]{:S(2)}) %all-to-all-start.1) | async-done | bytes 327712 | tf_op jit(solution)/shard_map/all_to_all | solution.py:586
  43.6 0.8 piece.4
  44.4 3.6 %all-to-all-start.2 = ((f32[8,10,8,128]{3,2,1,0:T(8,128)}), f32[8,10,8,128]{3,2,1,0:T(8,128)S(1)}, u32[]{:S(2)}, u32[]{:S(2)}) async-start(f32[8,10,8,128]{3,2,1,0:T(8,128)} %piece.4), calls=%async_computation.2 | async-start | bytes 655360 | tf_op jit(solution)/shard_map/all_to_all | solution.py:615
  48.5 7.4 %hidden.9 = (f32[20,16,128]{2,1,0:T(8,128)S(1)}, f32[8,128]{1,0:T(8,128)S(1)}, f32[10,256,512]{2,1,0:T(8,128)}, f32[10,256,512]{2,1,0:T(8,128)}) custom-call(s32[20]{0:T(128)S(1)} %bitcast.68, f32[56,128]{1,0:T(8,128)S(1)} %get-tuple-element.95.refs_1_.refs_3_, ...), custom_call_target="tpu_custom_call", output_to_operand_aliasing={{2}: (11, {}), {3}: (12, {})} | custom-call | flops 2013265920 | bytes 20971520 | tf_op jit(solution)/shard_map/hidden/pallas_call | solution.py:89
  56.5 2.0 all-to-all-done.2
  58.5 1.8 pack.4
  60.3 4.4 %all-to-all-start.3 = ((f32[32,1,128]{2,1,0:T(1,128)}), f32[32,1,128]{2,1,0:T(1,128)S(1)}, u32[]{:S(2)}, u32[]{:S(2)}) async-start(f32[32,1,128]{2,1,0:T(1,128)} %pack.4), calls=%async_computation.3 | async-start | bytes 32768 | tf_op jit(solution)/shard_map/all_to_all | solution.py:548
  64.7 7.1 %all-to-all-done.3.refs_0_ = f32[32,1,128]{2,1,0:T(1,128)S(1)} async-done(((f32[32,1,128]{2,1,0:T(1,128)}), f32[32,1,128]{2,1,0:T(1,128)S(1)}, u32[]{:S(2)}, u32[]{:S(2)}) %all-to-all-start.3) | async-done | bytes 16416 | tf_op jit(solution)/shard_map/all_to_all | solution.py:548
  71.7 8.8 %update.4 = (f32[256,256]{1,0:T(8,128)S(1)}, f32[40,16,128]{2,1,0:T(8,128)}, f32[256,256]{1,0:T(8,128)S(1)}, f32[56,128]{1,0:T(8,128)S(1)}, f32[10,256,512]{2,1,0:T(8,128)}) custom-call(f32[32,1,128]{2,1,0:T(1,128)S(1)} %all-to-all-done.3.refs_0_, f32[256,256]{1,0:T(8,128)S(1)} %maximum_select_fusion.refs_1_, ...), custom_call_target="tpu_custom_call" | custom-call | flops 10485760 | bytes 20971520 | tf_op jit(solution)/shard_map/update/pallas_call | solution.py:89
  80.6 3.4 %all-to-all-start.4 = ((f32[8,10,8,128]{3,2,1,0:T(8,128)}), f32[8,10,8,128]{3,2,1,0:T(8,128)S(1)}, u32[]{:S(2)}, u32[]{:S(2)}) async-start(f32[8,10,8,128]{3,2,1,0:T(8,128)} %bitcast.9), calls=%async_computation.4 | async-start | bytes 655360 | tf_op jit(solution)/shard_map/all_to_all | solution.py:586
  84.1 8.3 %hidden.10 = (f32[20,16,128]{2,1,0:T(8,128)S(1)}, f32[8,128]{1,0:T(8,128)S(1)}, f32[10,256,512]{2,1,0:T(8,128)}, f32[10,256,512]{2,1,0:T(8,128)}) custom-call(s32[20]{0:T(128)S(1)} %bitcast.69, f32[56,128]{1,0:T(8,128)S(1)} %get-tuple-element.116.refs_1_.refs_3_, f32[256,256]{1,0:T(8,128)S(1)} %get-tuple-element.117.refs_2_.refs_4_, ...), custom_call_target="tpu_custom_call" | custom-call | flops 2013265920 | bytes 20971520 | tf_op jit(solution)/shard_map/hidden/pallas_call | solution.py:89
  92.4 2.1 all-to-all-done.4.recv_ref
  94.6 0.8 piece.5
  95.3 3.7 %all-to-all-start.5 = ((f32[8,10,8,128]{3,2,1,0:T(8,128)}), f32[8,10,8,128]{3,2,1,0:T(8,128)S(1)}, u32[]{:S(2)}, u32[]{:S(2)}) async-start(f32[8,10,8,128]{3,2,1,0:T(8,128)} %piece.5), calls=%async_computation.5 | async-start | bytes 655360 | tf_op jit(solution)/shard_map/all_to_all | solution.py:615
  99.7 8.2 %hidden.11 = (f32[20,16,128]{2,1,0:T(8,128)S(1)}, f32[8,128]{1,0:T(8,128)S(1)}, f32[10,256,512]{2,1,0:T(8,128)}, f32[10,256,512]{2,1,0:T(8,128)}) custom-call(s32[20]{0:T(128)S(1)} %bitcast.70, f32[56,128]{1,0:T(8,128)S(1)} %get-tuple-element.116.refs_1_.refs_3_, ...), custom_call_target="tpu_custom_call", output_to_operand_aliasing={{2}: (12, {}), {3}: (13, {})} | custom-call | flops 2013265920 | bytes 20971520 | tf_op jit(solution)/shard_map/hidden/pallas_call | solution.py:89
  108.6 1.4 all-to-all-done.5
  110.0 1.8 pack.5
  111.8 4.7 %all-to-all-start.6 = ((f32[32,1,128]{2,1,0:T(1,128)}), f32[32,1,128]{2,1,0:T(1,128)S(1)}, u32[]{:S(2)}, u32[]{:S(2)}) async-start(f32[32,1,128]{2,1,0:T(1,128)} %pack.5), calls=%async_computation.6 | async-start | bytes 32768 | tf_op jit(solution)/shard_map/all_to_all | solution.py:548
  116.6 7.1 %all-to-all-done.6.refs_0_ = f32[32,1,128]{2,1,0:T(1,128)S(1)} async-done(((f32[32,1,128]{2,1,0:T(1,128)}), f32[32,1,128]{2,1,0:T(1,128)S(1)}, u32[]{:S(2)}, u32[]{:S(2)}) %all-to-all-start.6) | async-done | bytes 16416 | tf_op jit(solution)/shard_map/all_to_all | solution.py:548
  123.6 8.8 %update.5 = (f32[256,256]{1,0:T(8,128)S(1)}, f32[40,16,128]{2,1,0:T(8,128)}, f32[256,256]{1,0:T(8,128)S(1)}, f32[56,128]{1,0:T(8,128)S(1)}, f32[10,256,512]{2,1,0:T(8,128)}) custom-call(f32[32,1,128]{2,1,0:T(1,128)S(1)} %all-to-all-done.6.refs_0_, f32[256,256]{1,0:T(8,128)S(1)} %maximum_select_fusion.1.refs_1_, ...), custom_call_target="tpu_custom_call" | custom-call | flops 10485760 | bytes 20971520 | tf_op jit(solution)/shard_map/update/pallas_call | solution.py:89
  132.5 3.4 %all-to-all-start.7 = ((f32[8,10,8,128]{3,2,1,0:T(8,128)}), f32[8,10,8,128]{3,2,1,0:T(8,128)S(1)}, u32[]{:S(2)}, u32[]{:S(2)}) async-start(f32[8,10,8,128]{3,2,1,0:T(8,128)} %bitcast.11), calls=%async_computation.7 | async-start | bytes 655360 | tf_op jit(solution)/shard_map/all_to_all | solution.py:586
  136.0 9.2 %hidden.12 = (f32[20,16,128]{2,1,0:T(8,128)S(1)}, f32[8,128]{1,0:T(8,128)S(1)}, f32[10,256,512]{2,1,0:T(8,128)}, f32[10,256,512]{2,1,0:T(8,128)}) custom-call(s32[20]{0:T(128)S(1)} %bitcast.71, f32[56,128]{1,0:T(8,128)S(1)} %get-tuple-element.137.refs_1_.refs_3_, f32[256,256]{1,0:T(8,128)S(1)} %get-tuple-element.138.refs_2_.refs_4_, ...), custom_call_target="tpu_custom_call" | custom-call | flops 2013265920 | bytes 20971520 | tf_op jit(solution)/shard_map/hidden/pallas_call | solution.py:89
  145.2 1.2 all-to-all-done.7.recv_ref
  146.4 0.8 piece.6
  147.2 4.6 %all-to-all-start.8 = ((f32[8,10,8,128]{3,2,1,0:T(8,128)}), f32[8,10,8,128]{3,2,1,0:T(8,128)S(1)}, u32[]{:S(2)}, u32[]{:S(2)}) async-start(f32[8,10,8,128]{3,2,1,0:T(8,128)} %piece.6), calls=%async_computation.8 | async-start | bytes 655360 | tf_op jit(solution)/shard_map/all_to_all | solution.py:615
  152.5 9.1 %hidden.13 = (f32[20,16,128]{2,1,0:T(8,128)S(1)}, f32[8,128]{1,0:T(8,128)S(1)}, f32[10,256,512]{2,1,0:T(8,128)}, f32[10,256,512]{2,1,0:T(8,128)}) custom-call(s32[20]{0:T(128)S(1)} %bitcast.72, f32[56,128]{1,0:T(8,128)S(1)} %get-tuple-element.137.refs_1_.refs_3_, ...), custom_call_target="tpu_custom_call", output_to_operand_aliasing={{2}: (13, {}), {3}: (14, {})} | custom-call | flops 2013265920 | bytes 20971520 | tf_op jit(solution)/shard_map/hidden/pallas_call | solution.py:89
  162.8 1.8 pack.6
  164.6 5.7 %all-to-all-start.9 = ((f32[32,1,128]{2,1,0:T(1,128)}), f32[32,1,128]{2,1,0:T(1,128)S(1)}, u32[]{:S(2)}, u32[]{:S(2)}) async-start(f32[32,1,128]{2,1,0:T(1,128)} %pack.6), calls=%async_computation.9 | async-start | bytes 32768 | tf_op jit(solution)/shard_map/all_to_all | solution.py:548
  170.3 7.1 %all-to-all-done.9.refs_0_ = f32[32,1,128]{2,1,0:T(1,128)S(1)} async-done(((f32[32,1,128]{2,1,0:T(1,128)}), f32[32,1,128]{2,1,0:T(1,128)S(1)}, u32[]{:S(2)}, u32[]{:S(2)}) %all-to-all-start.9) | async-done | bytes 16416 | tf_op jit(solution)/shard_map/all_to_all | solution.py:548
  177.3 8.8 %update.6 = (f32[256,256]{1,0:T(8,128)S(1)}, f32[40,16,128]{2,1,0:T(8,128)}, f32[256,256]{1,0:T(8,128)S(1)}, f32[56,128]{1,0:T(8,128)S(1)}, f32[10,256,512]{2,1,0:T(8,128)}) custom-call(f32[32,1,128]{2,1,0:T(1,128)S(1)} %all-to-all-done.9.refs_0_, f32[256,256]{1,0:T(8,128)S(1)} %maximum_select_fusion.2.refs_1_, ...), custom_call_target="tpu_custom_call" | custom-call | flops 10485760 | bytes 20971520 | tf_op jit(solution)/shard_map/update/pallas_call | solution.py:89
  186.2 3.4 %all-to-all-start.10 = ((f32[8,10,8,128]{3,2,1,0:T(8,128)}), f32[8,10,8,128]{3,2,1,0:T(8,128)S(1)}, u32[]{:S(2)}, u32[]{:S(2)}) async-start(f32[8,10,8,128]{3,2,1,0:T(8,128)} %bitcast.13), calls=%async_computation.10 | async-start | bytes 655360 | tf_op jit(solution)/shard_map/all_to_all | solution.py:586
  189.7 9.7 %hidden.14 = (f32[20,16,128]{2,1,0:T(8,128)S(1)}, f32[8,128]{1,0:T(8,128)S(1)}, f32[10,256,512]{2,1,0:T(8,128)}, f32[10,256,512]{2,1,0:T(8,128)}) custom-call(s32[20]{0:T(128)S(1)} %bitcast.73, f32[56,128]{1,0:T(8,128)S(1)} %get-tuple-element.158.refs_1_.refs_3_, f32[256,256]{1,0:T(8,128)S(1)} %get-tuple-element.159.refs_2_.refs_4_, ...), custom_call_target="tpu_custom_call" | custom-call | flops 2013265920 | bytes 20971520 | tf_op jit(solution)/shard_map/hidden/pallas_call | solution.py:89
  199.5 0.7 all-to-all-done.10.recv_ref
  200.1 0.8 piece.7
  200.9 5.2 %all-to-all-start.11 = ((f32[8,10,8,128]{3,2,1,0:T(8,128)}), f32[8,10,8,128]{3,2,1,0:T(8,128)S(1)}, u32[]{:S(2)}, u32[]{:S(2)}) async-start(f32[8,10,8,128]{3,2,1,0:T(8,128)} %piece.7), calls=%async_computation.11 | async-start | bytes 655360 | tf_op jit(solution)/shard_map/all_to_all | solution.py:615
  206.8 9.7 %hidden.15 = (f32[20,16,128]{2,1,0:T(8,128)S(1)}, f32[8,128]{1,0:T(8,128)S(1)}, f32[10,256,512]{2,1,0:T(8,128)}, f32[10,256,512]{2,1,0:T(8,128)}) custom-call(s32[20]{0:T(128)S(1)} %bitcast.74, f32[56,128]{1,0:T(8,128)S(1)} %get-tuple-element.158.refs_1_.refs_3_, ...), custom_call_target="tpu_custom_call", output_to_operand_aliasing={{2}: (14, {}), {3}: (15, {})} | custom-call | flops 2013265920 | bytes 20971520 | tf_op jit(solution)/shard_map/hidden/pallas_call | solution.py:89
  217.1 1.8 pack.7
  218.9 6.1 %all-to-all-start.12 = ((f32[32,1,128]{2,1,0:T(1,128)}), f32[32,1,128]{2,1,0:T(1,128)S(1)}, u32[]{:S(2)}, u32[]{:S(2)}) async-start(f32[32,1,128]{2,1,0:T(1,128)} %pack.7), calls=%async_computation.12 | async-start | bytes 32768 | tf_op jit(solution)/shard_map/all_to_all | solution.py:548
  225.1 7.1 %all-to-all-done.12.refs_0_ = f32[32,1,128]{2,1,0:T(1,128)S(1)} async-done(((f32[32,1,128]{2,1,0:T(1,128)}), f32[32,1,128]{2,1,0:T(1,128)S(1)}, u32[]{:S(2)}, u32[]{:S(2)}) %all-to-all-start.12) | async-done | bytes 16416 | tf_op jit(solution)/shard_map/all_to_all | solution.py:548
  232.2 8.8 %update.7 = (f32[256,256]{1,0:T(8,128)}, f32[16,5120]{1,0:T(8,128)}, f32[256,5120]{1,0:T(8,128)}) custom-call(f32[32,1,128]{2,1,0:T(1,128)S(1)} %all-to-all-done.12.refs_0_, f32[256,256]{1,0:T(8,128)S(1)} %maximum_select_fusion.3.refs_1_, f32[5,8,128]{2,1,0:T(8,128)S(1)} %broadcast_in_dim.4.refs_1_.refs_2_, ...), custom_call_target="tpu_custom_call" | custom-call | flops 10485760 | bytes 20971520 | tf_op jit(solution)/shard_map/update/pallas_call | solution.py:89
  (74 shorter events, 6.1 us)
Async XLA Ops:
  0.6 21.5 %copy-start = (f32[16,5120]{1,0:T(8,128)S(1)}, f32[16,5120]{1,0:T(8,128)}, u32[]{:S(2)}) copy-start(f32[16,5120]{1,0:T(8,128)} %refs_4_.17) | copy-start | bytes 983044
  0.6 21.5 %copy-start.2 = (s32[5120]{0:T(1024)S(1)}, s32[5120]{0:T(1024)}, u32[]{:S(2)}) copy-start(s32[5120]{0:T(1024)} %param.17) | copy-start | bytes 61444
  0.7 32.4 %copy-start.14 = (s32[1,20]{1,0:T(1,128)S(1)}, s32[1,20]{1,0:T(1,128)}, u32[]{:S(2)}) copy-start(s32[1,20]{1,0:T(1,128)} %param.16) | copy-start | bytes 244
  0.7 21.5 %copy-start.1 = (f32[5120]{0:T(1024)S(1)}, f32[5120]{0:T(1024)}, u32[]{:S(2)}) copy-start(f32[5120]{0:T(1024)} %param.13) | copy-start | bytes 61444
  0.7 21.5 %copy-start.3 = (f32[5120]{0:T(1024)S(1)}, f32[5120]{0:T(1024)}, u32[]{:S(2)}) copy-start(f32[5120]{0:T(1024)} %param.12) | copy-start | bytes 61444
  0.7 21.5 %copy-start.4 = (f32[16,16,256]{2,1,0:T(8,128)S(1)}, f32[16,16,256]{2,1,0:T(8,128)}, u32[]{:S(2)}) copy-start(f32[16,16,256]{2,1,0:T(8,128)} %param.10) | copy-start | bytes 786436
  0.7 13.3 %copy-start.15 = (s32[5]{0:T(128)S(1)}, s32[5]{0:T(128)}, u32[]{:S(2)}) copy-start(s32[5]{0:T(128)} %param.19) | copy-start | bytes 64
  0.7 13.3 %copy-start.16 = (s32[5]{0:T(128)S(1)}, s32[5]{0:T(128)}, u32[]{:S(2)}) copy-start(s32[5]{0:T(128)} %param.18) | copy-start | bytes 64
  6.6 15.5 %all-to-all-start = ((f32[32,8,128]{2,1,0:T(8,128)}), f32[32,8,128]{2,1,0:T(8,128)S(1)}, u32[]{:S(2)}, u32[]{:S(2)}) async-start(f32[32,8,128]{2,1,0:T(8,128)} %get-tuple-element.92), calls=%async_computation | async-start | bytes 262144 | tf_op jit(solution)/shard_map/all_to_all | solution.py:548
  22.2 1.0 copy-start.5
  29.3 14.3 %all-to-all-start.1 = ((f32[8,10,8,128]{3,2,1,0:T(8,128)}), f32[8,10,8,128]{3,2,1,0:T(8,128)S(1)}, u32[]{:S(2)}, u32[]{:S(2)}) async-start(f32[8,10,8,128]{3,2,1,0:T(8,128)} %bitcast.7), calls=%async_computation.1 | async-start | bytes 655360 | tf_op jit(solution)/shard_map/all_to_all | solution.py:586
  32.8 15.2 %collective-permute-start = (f32[256,256]{1,0:T(8,128)S(1)}, f32[256,256]{1,0:T(8,128)S(1)}, u32[]{:S(2)}, u32[]{:S(2)}) collective-permute-start(f32[256,256]{1,0:T(8,128)S(1)} %get-tuple-element.102), channel_id=1, source_target_pairs={{0,1},{1,0},{2,3},{3,2},{4,5},{5,4},{6,7},{7,6},{8,9},{9,8},{10,11... | collective-permute-start | bytes 786440 | tf_op jit(solution)/shard_map/ppermute | solution.py:587
  40.4 0.7 copy-start.6
  44.4 14.1 %all-to-all-start.2 = ((f32[8,10,8,128]{3,2,1,0:T(8,128)}), f32[8,10,8,128]{3,2,1,0:T(8,128)S(1)}, u32[]{:S(2)}, u32[]{:S(2)}) async-start(f32[8,10,8,128]{3,2,1,0:T(8,128)} %piece.4), calls=%async_computation.2 | async-start | bytes 655360 | tf_op jit(solution)/shard_map/all_to_all | solution.py:615
  48.1 7.8 %collective-permute-start.1 = (f32[128,256]{1,0:T(8,128)S(1)}, f32[128,256]{1,0:T(8,128)S(1)}, u32[]{:S(2)}, u32[]{:S(2)}) collective-permute-start(f32[128,256]{1,0:T(8,128)S(1)} %dynamic-slice_add_fusion.3.near_ref), channel_id=1, source_target_pairs={{0,2},{1,3},{2,0},{3,1},{4,6},{5,7},{6,4},{7,5},{8,10},{9,11},{10,... | collective-permute-start | bytes 393224 | tf_op jit(solution)/shard_map/ppermute | solution.py:624
  55.8 0.7 copy-start.11
  56.5 8.1 %collective-permute-start.2 = (f32[128,256]{1,0:T(8,128)S(1)}, f32[128,256]{1,0:T(8,128)S(1)}, u32[]{:S(2)}, u32[]{:S(2)}) collective-permute-start(f32[128,256]{1,0:T(8,128)S(1)} %get-tuple-element.112), channel_id=1, source_target_pairs={{0,1},{1,0},{2,3},{3,2},{4,5},{5,4},{6,7},{7,6},{8,9},{9,8},{10,11... | collective-permute-start | bytes 393224 | tf_op jit(solution)/shard_map/ppermute | solution.py:635
  60.3 11.5 %all-to-all-start.3 = ((f32[32,1,128]{2,1,0:T(1,128)}), f32[32,1,128]{2,1,0:T(1,128)S(1)}, u32[]{:S(2)}, u32[]{:S(2)}) async-start(f32[32,1,128]{2,1,0:T(1,128)} %pack.4), calls=%async_computation.3 | async-start | bytes 32768 | tf_op jit(solution)/shard_map/all_to_all | solution.py:548
  80.6 14.0 %all-to-all-start.4 = ((f32[8,10,8,128]{3,2,1,0:T(8,128)}), f32[8,10,8,128]{3,2,1,0:T(8,128)S(1)}, u32[]{:S(2)}, u32[]{:S(2)}) async-start(f32[8,10,8,128]{3,2,1,0:T(8,128)} %bitcast.9), calls=%async_computation.4 | async-start | bytes 655360 | tf_op jit(solution)/shard_map/all_to_all | solution.py:586
  84.0 15.0 %collective-permute-start.3 = (f32[256,256]{1,0:T(8,128)S(1)}, f32[256,256]{1,0:T(8,128)S(1)}, u32[]{:S(2)}, u32[]{:S(2)}) collective-permute-start(f32[256,256]{1,0:T(8,128)S(1)} %get-tuple-element.123), channel_id=1, source_target_pairs={{0,1},{1,0},{2,3},{3,2},{4,5},{5,4},{6,7},{7,6},{8,9},{9,8},{10,11... | collective-permute-start | bytes 786440 | tf_op jit(solution)/shard_map/ppermute | solution.py:587
  92.4 6.6 %copy-start.8 = (f32[20,16,128]{2,1,0:T(8,128)}, f32[20,16,128]{2,1,0:T(8,128)S(1)}, u32[]{:S(2)}) copy-start(f32[20,16,128]{2,1,0:T(8,128)S(1)} %get-tuple-element.131.refs_3_) | copy-start | bytes 491524
  95.3 14.7 %all-to-all-start.5 = ((f32[8,10,8,128]{3,2,1,0:T(8,128)}), f32[8,10,8,128]{3,2,1,0:T(8,128)S(1)}, u32[]{:S(2)}, u32[]{:S(2)}) async-start(f32[8,10,8,128]{3,2,1,0:T(8,128)} %piece.5), calls=%async_computation.5 | async-start | bytes 655360 | tf_op jit(solution)/shard_map/all_to_all | solution.py:615
  99.1 8.8 %collective-permute-start.4 = (f32[128,256]{1,0:T(8,128)S(1)}, f32[128,256]{1,0:T(8,128)S(1)}, u32[]{:S(2)}, u32[]{:S(2)}) collective-permute-start(f32[128,256]{1,0:T(8,128)S(1)} %dynamic-slice_add_fusion.2.near_ref), channel_id=1, source_target_pairs={{0,2},{1,3},{2,0},{3,1},{4,6},{5,7},{6,4},{7,5},{8,10},{9,11},{10,... | collective-permute-start | bytes 393224 | tf_op jit(solution)/shard_map/ppermute | solution.py:624
  107.9 0.7 copy-start.12
  108.6 8.0 %collective-permute-start.5 = (f32[128,256]{1,0:T(8,128)S(1)}, f32[128,256]{1,0:T(8,128)S(1)}, u32[]{:S(2)}, u32[]{:S(2)}) collective-permute-start(f32[128,256]{1,0:T(8,128)S(1)} %get-tuple-element.133), channel_id=1, source_target_pairs={{0,1},{1,0},{2,3},{3,2},{4,5},{5,4},{6,7},{7,6},{8,9},{9,8},{10,11... | collective-permute-start | bytes 393224 | tf_op jit(solution)/shard_map/ppermute | solution.py:635
  111.8 11.8 %all-to-all-start.6 = ((f32[32,1,128]{2,1,0:T(1,128)}), f32[32,1,128]{2,1,0:T(1,128)S(1)}, u32[]{:S(2)}, u32[]{:S(2)}) async-start(f32[32,1,128]{2,1,0:T(1,128)} %pack.5), calls=%async_computation.6 | async-start | bytes 32768 | tf_op jit(solution)/shard_map/all_to_all | solution.py:548
  132.5 14.0 %all-to-all-start.7 = ((f32[8,10,8,128]{3,2,1,0:T(8,128)}), f32[8,10,8,128]{3,2,1,0:T(8,128)S(1)}, u32[]{:S(2)}, u32[]{:S(2)}) async-start(f32[8,10,8,128]{3,2,1,0:T(8,128)} %bitcast.11), calls=%async_computation.7 | async-start | bytes 655360 | tf_op jit(solution)/shard_map/all_to_all | solution.py:586
  135.9 15.9 %collective-permute-start.6 = (f32[256,256]{1,0:T(8,128)S(1)}, f32[256,256]{1,0:T(8,128)S(1)}, u32[]{:S(2)}, u32[]{:S(2)}) collective-permute-start(f32[256,256]{1,0:T(8,128)S(1)} %get-tuple-element.144), channel_id=1, source_target_pairs={{0,1},{1,0},{2,3},{3,2},{4,5},{5,4},{6,7},{7,6},{8,9},{9,8},{10,11... | collective-permute-start | bytes 786440 | tf_op jit(solution)/shard_map/ppermute | solution.py:587
  145.2 6.6 %copy-start.9 = (f32[20,16,128]{2,1,0:T(8,128)}, f32[20,16,128]{2,1,0:T(8,128)S(1)}, u32[]{:S(2)}) copy-start(f32[20,16,128]{2,1,0:T(8,128)S(1)} %get-tuple-element.152.refs_3_) | copy-start | bytes 491524
  147.2 15.6 %all-to-all-start.8 = ((f32[8,10,8,128]{3,2,1,0:T(8,128)}), f32[8,10,8,128]{3,2,1,0:T(8,128)S(1)}, u32[]{:S(2)}, u32[]{:S(2)}) async-start(f32[8,10,8,128]{3,2,1,0:T(8,128)} %piece.6), calls=%async_computation.8 | async-start | bytes 655360 | tf_op jit(solution)/shard_map/all_to_all | solution.py:615
  151.9 9.7 %collective-permute-start.7 = (f32[128,256]{1,0:T(8,128)S(1)}, f32[128,256]{1,0:T(8,128)S(1)}, u32[]{:S(2)}, u32[]{:S(2)}) collective-permute-start(f32[128,256]{1,0:T(8,128)S(1)} %dynamic-slice_add_fusion.1.near_ref), channel_id=1, source_target_pairs={{0,2},{1,3},{2,0},{3,1},{4,6},{5,7},{6,4},{7,5},{8,10},{9,11},{10,... | collective-permute-start | bytes 393224 | tf_op jit(solution)/shard_map/ppermute | solution.py:624
  161.6 0.7 copy-start.13
  162.3 8.0 %collective-permute-start.8 = (f32[128,256]{1,0:T(8,128)S(1)}, f32[128,256]{1,0:T(8,128)S(1)}, u32[]{:S(2)}, u32[]{:S(2)}) collective-permute-start(f32[128,256]{1,0:T(8,128)S(1)} %get-tuple-element.154), channel_id=1, source_target_pairs={{0,1},{1,0},{2,3},{3,2},{4,5},{5,4},{6,7},{7,6},{8,9},{9,8},{10,11... | collective-permute-start | bytes 393224 | tf_op jit(solution)/shard_map/ppermute | solution.py:635
  164.6 12.8 %all-to-all-start.9 = ((f32[32,1,128]{2,1,0:T(1,128)}), f32[32,1,128]{2,1,0:T(1,128)S(1)}, u32[]{:S(2)}, u32[]{:S(2)}) async-start(f32[32,1,128]{2,1,0:T(1,128)} %pack.6), calls=%async_computation.9 | async-start | bytes 32768 | tf_op jit(solution)/shard_map/all_to_all | solution.py:548
  186.2 14.0 %all-to-all-start.10 = ((f32[8,10,8,128]{3,2,1,0:T(8,128)}), f32[8,10,8,128]{3,2,1,0:T(8,128)S(1)}, u32[]{:S(2)}, u32[]{:S(2)}) async-start(f32[8,10,8,128]{3,2,1,0:T(8,128)} %bitcast.13), calls=%async_computation.10 | async-start | bytes 655360 | tf_op jit(solution)/shard_map/all_to_all | solution.py:586
  189.6 16.5 %collective-permute-start.9 = (f32[256,256]{1,0:T(8,128)S(1)}, f32[256,256]{1,0:T(8,128)S(1)}, u32[]{:S(2)}, u32[]{:S(2)}) collective-permute-start(f32[256,256]{1,0:T(8,128)S(1)} %get-tuple-element.165), channel_id=1, source_target_pairs={{0,1},{1,0},{2,3},{3,2},{4,5},{5,4},{6,7},{7,6},{8,9},{9,8},{10,11... | collective-permute-start | bytes 786440 | tf_op jit(solution)/shard_map/ppermute | solution.py:587
  199.5 6.6 %copy-start.7 = (f32[20,16,128]{2,1,0:T(8,128)}, f32[20,16,128]{2,1,0:T(8,128)S(1)}, u32[]{:S(2)}) copy-start(f32[20,16,128]{2,1,0:T(8,128)S(1)} %get-tuple-element.173.refs_3_) | copy-start | bytes 491524
  200.9 16.2 %all-to-all-start.11 = ((f32[8,10,8,128]{3,2,1,0:T(8,128)}), f32[8,10,8,128]{3,2,1,0:T(8,128)S(1)}, u32[]{:S(2)}, u32[]{:S(2)}) async-start(f32[8,10,8,128]{3,2,1,0:T(8,128)} %piece.7), calls=%async_computation.11 | async-start | bytes 655360 | tf_op jit(solution)/shard_map/all_to_all | solution.py:615
  206.1 10.3 %collective-permute-start.10 = (f32[128,256]{1,0:T(8,128)S(1)}, f32[128,256]{1,0:T(8,128)S(1)}, u32[]{:S(2)}, u32[]{:S(2)}) collective-permute-start(f32[128,256]{1,0:T(8,128)S(1)} %dynamic-slice_add_fusion.near_ref), channel_id=1, source_target_pairs={{0,2},{1,3},{2,0},{3,1},{4,6},{5,7},{6,4},{7,5},{8,10},{9,11},{10,... | collective-permute-start | bytes 393224 | tf_op jit(solution)/shard_map/ppermute | solution.py:624
  216.5 0.7 copy-start.10
  217.1 7.9 %collective-permute-start.11 = (f32[128,256]{1,0:T(8,128)S(1)}, f32[128,256]{1,0:T(8,128)S(1)}, u32[]{:S(2)}, u32[]{:S(2)}) collective-permute-start(f32[128,256]{1,0:T(8,128)S(1)} %get-tuple-element.175), channel_id=1, source_target_pairs={{0,1},{1,0},{2,3},{3,2},{4,5},{5,4},{6,7},{7,6},{8,9},{9,8},{10,11... | collective-permute-start | bytes 393224 | tf_op jit(solution)/shard_map/ppermute | solution.py:635
  218.9 13.2 %all-to-all-start.12 = ((f32[32,1,128]{2,1,0:T(1,128)}), f32[32,1,128]{2,1,0:T(1,128)S(1)}, u32[]{:S(2)}, u32[]{:S(2)}) async-start(f32[32,1,128]{2,1,0:T(1,128)} %pack.7), calls=%async_computation.12 | async-start | bytes 32768 | tf_op jit(solution)/shard_map/all_to_all | solution.py:548

commit v3 on v2

--- a/solution.py
+++ b/solution.py
@@ -561,7 +561,7 @@
     recv = exchange(packed)
 
     col_sums, prices, totals, coef, dispatch = staged_call(
-        functools.partial(start_body, dims), [], [recv], [sizes, load, base] + vector, [],
+        functools.partial(start_body, dims), [], [recv], [sizes, far_away(load), far_away(base)] + vector, [],
         [col_shape, grid_shape, grid_shape, coef_shape], [state], [buffer, dma((chunks,))],
         "start",
     )
@@ -638,7 +638,7 @@
         )
 
         (packed,) = staged_call(
-            functools.partial(pack_body, dims), [], [plan, primal, partial], [far_away(v) for v in cols], [],
+            functools.partial(pack_body, dims), [], [plan, primal], [far_away(v) for v in (partial, *cols)], [],
             [shape((devices, 1, LANES), F32)], [], [], "pack", limit=4,
         )
         recv = exchange(packed)

time: 242 us -> 242 us (level)
  no operation moved by 1% of the time
where the time goes in v3:
time: 242 us; the launch traced here: 241 us
  Pallas kernels  128 us (53%)
  starting transfers between devices  61.8 us (26%)
  waiting for transfers between devices  46.8 us (19%)
  local copies, waits for them, and re-layouts  2.88 us (1%)
    pallas_call x18, Pallas kernels, staged_call(): pl.pallas_call(stage(body, len(near), len(small), len(large), len(small_o...  124 us
    all_to_all x5, waiting for transfers between devices, exchange(): return lax.all_to_all(x, ('scen', 'gen'), 0, 0)  36.3 us
    all_to_all x5, starting transfers between devices, exchange(): return lax.all_to_all(x, ('scen', 'gen'), 0, 0)  28.2 us
    all_to_all x4, starting transfers between devices, local(): gathered = lax.all_to_all(piece, 'scen', 0, 0)  17.2 us
    all_to_all x4, starting transfers between devices, local(): got = lax.all_to_all(flat, 'scen', 0, 0)  13.8 us
    all_to_all x4, waiting for transfers between devices, local(): got = lax.all_to_all(flat, 'scen', 0, 0)  6.58 us
  transfers between devices with their start and end apart: 25, of which 12 were waited for; matrix products, arithmetic and copies ran while one was open for 0% of the time, Pallas kernels for 33%

profile of v3, /device:TPU:0, one launch (start us, length us, event | category | flops | bytes accessed | tf_op | source)
XLA Modules:
  0.0 241.0 jit_solution(6461971288107636597)
XLA Ops:
  0.7 5.9 %first.1 = (f32[16,5120]{1,0:T(8,128)}, f32[32,8,128]{2,1,0:T(8,128)}) custom-call(s32[20]{0:T(128)} %bitcast.63, f32[256,256]{1,0:T(8,128)} %bitcast.90, f32[16,5120]{1,0:T(8,128)} %refs_4_.17, f32[1,5120]{1,0:T(1,128)} %bitcast.53, f32[1,5120]{1,0:T(1,128)} %bitcast.17, s32[1,5120]{1,0:T(1,128)} %bitcast.31, bf16[10,2,256,256]{3,2,1,0:T(8,128)(2,1)} %bitcast.72, ...), custom_call_target="tpu_custom_call" | custom-call | tf_op jit(solution)/shard_map/first/pallas_call | solution.py:89
  6.6 7.3 %all-to-all-start = ((f32[32,8,128]{2,1,0:T(8,128)}), f32[32,8,128]{2,1,0:T(8,128)S(1)}, u32[]{:S(2)}, u32[]{:S(2)}) async-start(f32[32,8,128]{2,1,0:T(8,128)} %get-tuple-element.92), calls=%async_computation | async-start | bytes 262144 | tf_op jit(solution)/shard_map/all_to_all | solution.py:548
  14.0 8.1 %all-to-all-done.refs_0_ = f32[32,8,128]{2,1,0:T(8,128)S(1)} async-done(((f32[32,8,128]{2,1,0:T(8,128)}), f32[32,8,128]{2,1,0:T(8,128)S(1)}, u32[]{:S(2)}, u32[]{:S(2)}) %all-to-all-start) | async-done | bytes 131104 | tf_op jit(solution)/shard_map/all_to_all | solution.py:548
  22.2 6.9 %start.1 = (f32[40,16,128]{2,1,0:T(8,128)}, f32[256,256]{1,0:T(8,128)S(1)}, f32[256,256]{1,0:T(8,128)S(1)}, f32[56,128]{1,0:T(8,128)S(1)}, f32[10,256,512]{2,1,0:T(8,128)}) custom-call(f32[32,8,128]{2,1,0:T(8,128)S(1)} %all-to-all-done.refs_0_, f32[5,8,128]{2,1,0:T(8,128)S(1)} %broadcast_in_dim.4.refs_1_.refs_2_, f32[256,256]{1,0:T(8,128)} %bitcast.91, ...), custom_call_target="tpu_custom_call" | custom-call | tf_op jit(solution)/shard_map/start/pallas_call | solution.py:89
  29.1 3.4 %all-to-all-start.1 = ((f32[8,10,8,128]{3,2,1,0:T(8,128)}), f32[8,10,8,128]{3,2,1,0:T(8,128)S(1)}, u32[]{:S(2)}, u32[]{:S(2)}) async-start(f32[8,10,8,128]{3,2,1,0:T(8,128)} %bitcast.7), calls=%async_computation.1 | async-start | bytes 655360 | tf_op jit(solution)/shard_map/all_to_all | solution.py:586
  32.8 7.4 %hidden.8 = (f32[20,16,128]{2,1,0:T(8,128)S(1)}, f32[8,128]{1,0:T(8,128)S(1)}, f32[10,256,512]{2,1,0:T(8,128)}, f32[10,256,512]{2,1,0:T(8,128)}) custom-call(s32[20]{0:T(128)S(1)} %bitcast.64, f32[56,128]{1,0:T(8,128)S(1)} %get-tuple-element.95.refs_1_.refs_3_, f32[256,256]{1,0:T(8,128)S(1)} %get-tuple-element.96.refs_2_.refs_4_, ...), custom_call_target="tpu_custom_call" | custom-call | flops 2013265920 | bytes 20971520 | tf_op jit(solution)/shard_map/hidden/pallas_call | solution.py:89
  40.2 0.7 copy-done.4
  40.9 2.5 %all-to-all-done.1.recv_ref = f32[8,10,8,128]{3,2,1,0:T(8,128)S(1)} async-done(((f32[8,10,8,128]{3,2,1,0:T(8,128)}), f32[8,10,8,128]{3,2,1,0:T(8,128)S(1)}, u32[]{:S(2)}, u32[]{:S(2)}) %all-to-all-start.1) | async-done | bytes 327712 | tf_op jit(solution)/shard_map/all_to_all | solution.py:586
  43.4 0.8 piece.4
  44.2 3.6 %all-to-all-start.2 = ((f32[8,10,8,128]{3,2,1,0:T(8,128)}), f32[8,10,8,128]{3,2,1,0:T(8,128)S(1)}, u32[]{:S(2)}, u32[]{:S(2)}) async-start(f32[8,10,8,128]{3,2,1,0:T(8,128)} %piece.4), calls=%async_computation.2 | async-start | bytes 655360 | tf_op jit(solution)/shard_map/all_to_all | solution.py:615
  48.3 7.4 %hidden.9 = (f32[20,16,128]{2,1,0:T(8,128)S(1)}, f32[8,128]{1,0:T(8,128)S(1)}, f32[10,256,512]{2,1,0:T(8,128)}, f32[10,256,512]{2,1,0:T(8,128)}) custom-call(s32[20]{0:T(128)S(1)} %bitcast.65, f32[56,128]{1,0:T(8,128)S(1)} %get-tuple-element.95.refs_1_.refs_3_, ...), custom_call_target="tpu_custom_call", output_to_operand_aliasing={{2}: (11, {}), {3}: (12, {})} | custom-call | flops 2013265920 | bytes 20971520 | tf_op jit(solution)/shard_map/hidden/pallas_call | solution.py:89
  56.3 2.0 all-to-all-done.2
  58.3 1.8 pack.4
  60.1 4.3 %all-to-all-start.3 = ((f32[32,1,128]{2,1,0:T(1,128)}), f32[32,1,128]{2,1,0:T(1,128)S(1)}, u32[]{:S(2)}, u32[]{:S(2)}) async-start(f32[32,1,128]{2,1,0:T(1,128)} %pack.4), calls=%async_computation.3 | async-start | bytes 32768 | tf_op jit(solution)/shard_map/all_to_all | solution.py:548
  64.5 7.1 %all-to-all-done.3.refs_0_ = f32[32,1,128]{2,1,0:T(1,128)S(1)} async-done(((f32[32,1,128]{2,1,0:T(1,128)}), f32[32,1,128]{2,1,0:T(1,128)S(1)}, u32[]{:S(2)}, u32[]{:S(2)}) %all-to-all-start.3) | async-done | bytes 16416 | tf_op jit(solution)/shard_map/all_to_all | solution.py:548
  71.5 8.8 %update.4 = (f32[256,256]{1,0:T(8,128)S(1)}, f32[40,16,128]{2,1,0:T(8,128)}, f32[256,256]{1,0:T(8,128)S(1)}, f32[56,128]{1,0:T(8,128)S(1)}, f32[10,256,512]{2,1,0:T(8,128)}) custom-call(f32[32,1,128]{2,1,0:T(1,128)S(1)} %all-to-all-done.3.refs_0_, f32[256,256]{1,0:T(8,128)S(1)} %maximum_select_fusion.refs_1_, ...), custom_call_target="tpu_custom_call" | custom-call | flops 10485760 | bytes 20971520 | tf_op jit(solution)/shard_map/update/pallas_call | solution.py:89
  80.4 3.4 %all-to-all-start.4 = ((f32[8,10,8,128]{3,2,1,0:T(8,128)}), f32[8,10,8,128]{3,2,1,0:T(8,128)S(1)}, u32[]{:S(2)}, u32[]{:S(2)}) async-start(f32[8,10,8,128]{3,2,1,0:T(8,128)} %bitcast.9), calls=%async_computation.4 | async-start | bytes 655360 | tf_op jit(solution)/shard_map/all_to_all | solution.py:586
  83.9 8.3 %hidden.10 = (f32[20,16,128]{2,1,0:T(8,128)S(1)}, f32[8,128]{1,0:T(8,128)S(1)}, f32[10,256,512]{2,1,0:T(8,128)}, f32[10,256,512]{2,1,0:T(8,128)}) custom-call(s32[20]{0:T(128)S(1)} %bitcast.66, f32[56,128]{1,0:T(8,128)S(1)} %get-tuple-element.116.refs_1_.refs_3_, f32[256,256]{1,0:T(8,128)S(1)} %get-tuple-element.117.refs_2_.refs_4_, ...), custom_call_target="tpu_custom_call" | custom-call | flops 2013265920 | bytes 20971520 | tf_op jit(solution)/shard_map/hidden/pallas_call | solution.py:89
  92.2 2.2 all-to-all-done.4.recv_ref
  94.3 0.8 piece.5
  95.1 3.7 %all-to-all-start.5 = ((f32[8,10,8,128]{3,2,1,0:T(8,128)}), f32[8,10,8,128]{3,2,1,0:T(8,128)S(1)}, u32[]{:S(2)}, u32[]{:S(2)}) async-start(f32[8,10,8,128]{3,2,1,0:T(8,128)} %piece.5), calls=%async_computation.5 | async-start | bytes 655360 | tf_op jit(solution)/shard_map/all_to_all | solution.py:615
  99.5 8.2 %hidden.11 = (f32[20,16,128]{2,1,0:T(8,128)S(1)}, f32[8,128]{1,0:T(8,128)S(1)}, f32[10,256,512]{2,1,0:T(8,128)}, f32[10,256,512]{2,1,0:T(8,128)}) custom-call(s32[20]{0:T(128)S(1)} %bitcast.67, f32[56,128]{1,0:T(8,128)S(1)} %get-tuple-element.116.refs_1_.refs_3_, ...), custom_call_target="tpu_custom_call", output_to_operand_aliasing={{2}: (12, {}), {3}: (13, {})} | custom-call | flops 2013265920 | bytes 20971520 | tf_op jit(solution)/shard_map/hidden/pallas_call | solution.py:89
  108.4 1.4 all-to-all-done.5
  109.8 1.8 pack.5
  111.6 4.7 %all-to-all-start.6 = ((f32[32,1,128]{2,1,0:T(1,128)}), f32[32,1,128]{2,1,0:T(1,128)S(1)}, u32[]{:S(2)}, u32[]{:S(2)}) async-start(f32[32,1,128]{2,1,0:T(1,128)} %pack.5), calls=%async_computation.6 | async-start | bytes 32768 | tf_op jit(solution)/shard_map/all_to_all | solution.py:548
  116.3 7.1 %all-to-all-done.6.refs_0_ = f32[32,1,128]{2,1,0:T(1,128)S(1)} async-done(((f32[32,1,128]{2,1,0:T(1,128)}), f32[32,1,128]{2,1,0:T(1,128)S(1)}, u32[]{:S(2)}, u32[]{:S(2)}) %all-to-all-start.6) | async-done | bytes 16416 | tf_op jit(solution)/shard_map/all_to_all | solution.py:548
  123.4 8.8 %update.5 = (f32[256,256]{1,0:T(8,128)S(1)}, f32[40,16,128]{2,1,0:T(8,128)}, f32[256,256]{1,0:T(8,128)S(1)}, f32[56,128]{1,0:T(8,128)S(1)}, f32[10,256,512]{2,1,0:T(8,128)}) custom-call(f32[32,1,128]{2,1,0:T(1,128)S(1)} %all-to-all-done.6.refs_0_, f32[256,256]{1,0:T(8,128)S(1)} %maximum_select_fusion.1.refs_1_, ...), custom_call_target="tpu_custom_call" | custom-call | flops 10485760 | bytes 20971520 | tf_op jit(solution)/shard_map/update/pallas_call | solution.py:89
  132.3 3.4 %all-to-all-start.7 = ((f32[8,10,8,128]{3,2,1,0:T(8,128)}), f32[8,10,8,128]{3,2,1,0:T(8,128)S(1)}, u32[]{:S(2)}, u32[]{:S(2)}) async-start(f32[8,10,8,128]{3,2,1,0:T(8,128)} %bitcast.11), calls=%async_computation.7 | async-start | bytes 655360 | tf_op jit(solution)/shard_map/all_to_all | solution.py:586
  135.8 9.2 %hidden.12 = (f32[20,16,128]{2,1,0:T(8,128)S(1)}, f32[8,128]{1,0:T(8,128)S(1)}, f32[10,256,512]{2,1,0:T(8,128)}, f32[10,256,512]{2,1,0:T(8,128)}) custom-call(s32[20]{0:T(128)S(1)} %bitcast.68, f32[56,128]{1,0:T(8,128)S(1)} %get-tuple-element.137.refs_1_.refs_3_, f32[256,256]{1,0:T(8,128)S(1)} %get-tuple-element.138.refs_2_.refs_4_, ...), custom_call_target="tpu_custom_call" | custom-call | flops 2013265920 | bytes 20971520 | tf_op jit(solution)/shard_map/hidden/pallas_call | solution.py:89
  145.0 1.2 all-to-all-done.7.recv_ref
  146.2 0.8 piece.6
  147.0 4.6 %all-to-all-start.8 = ((f32[8,10,8,128]{3,2,1,0:T(8,128)}), f32[8,10,8,128]{3,2,1,0:T(8,128)S(1)}, u32[]{:S(2)}, u32[]{:S(2)}) async-start(f32[8,10,8,128]{3,2,1,0:T(8,128)} %piece.6), calls=%async_computation.8 | async-start | bytes 655360 | tf_op jit(solution)/shard_map/all_to_all | solution.py:615
  152.3 9.1 %hidden.13 = (f32[20,16,128]{2,1,0:T(8,128)S(1)}, f32[8,128]{1,0:T(8,128)S(1)}, f32[10,256,512]{2,1,0:T(8,128)}, f32[10,256,512]{2,1,0:T(8,128)}) custom-call(s32[20]{0:T(128)S(1)} %bitcast.69, f32[56,128]{1,0:T(8,128)S(1)} %get-tuple-element.137.refs_1_.refs_3_, ...), custom_call_target="tpu_custom_call", output_to_operand_aliasing={{2}: (13, {}), {3}: (14, {})} | custom-call | flops 2013265920 | bytes 20971520 | tf_op jit(solution)/shard_map/hidden/pallas_call | solution.py:89
  162.6 1.8 pack.6
  164.4 5.7 %all-to-all-start.9 = ((f32[32,1,128]{2,1,0:T(1,128)}), f32[32,1,128]{2,1,0:T(1,128)S(1)}, u32[]{:S(2)}, u32[]{:S(2)}) async-start(f32[32,1,128]{2,1,0:T(1,128)} %pack.6), calls=%async_computation.9 | async-start | bytes 32768 | tf_op jit(solution)/shard_map/all_to_all | solution.py:548
  170.1 7.1 %all-to-all-done.9.refs_0_ = f32[32,1,128]{2,1,0:T(1,128)S(1)} async-done(((f32[32,1,128]{2,1,0:T(1,128)}), f32[32,1,128]{2,1,0:T(1,128)S(1)}, u32[]{:S(2)}, u32[]{:S(2)}) %all-to-all-start.9) | async-done | bytes 16416 | tf_op jit(solution)/shard_map/all_to_all | solution.py:548
  177.1 8.8 %update.6 = (f32[256,256]{1,0:T(8,128)S(1)}, f32[40,16,128]{2,1,0:T(8,128)}, f32[256,256]{1,0:T(8,128)S(1)}, f32[56,128]{1,0:T(8,128)S(1)}, f32[10,256,512]{2,1,0:T(8,128)}) custom-call(f32[32,1,128]{2,1,0:T(1,128)S(1)} %all-to-all-done.9.refs_0_, f32[256,256]{1,0:T(8,128)S(1)} %maximum_select_fusion.2.refs_1_, ...), custom_call_target="tpu_custom_call" | custom-call | flops 10485760 | bytes 20971520 | tf_op jit(solution)/shard_map/update/pallas_call | solution.py:89
  186.0 3.4 %all-to-all-start.10 = ((f32[8,10,8,128]{3,2,1,0:T(8,128)}), f32[8,10,8,128]{3,2,1,0:T(8,128)S(1)}, u32[]{:S(2)}, u32[]{:S(2)}) async-start(f32[8,10,8,128]{3,2,1,0:T(8,128)} %bitcast.13), calls=%async_computation.10 | async-start | bytes 655360 | tf_op jit(solution)/shard_map/all_to_all | solution.py:586
  189.5 9.7 %hidden.14 = (f32[20,16,128]{2,1,0:T(8,128)S(1)}, f32[8,128]{1,0:T(8,128)S(1)}, f32[10,256,512]{2,1,0:T(8,128)}, f32[10,256,512]{2,1,0:T(8,128)}) custom-call(s32[20]{0:T(128)S(1)} %bitcast.70, f32[56,128]{1,0:T(8,128)S(1)} %get-tuple-element.158.refs_1_.refs_3_, f32[256,256]{1,0:T(8,128)S(1)} %get-tuple-element.159.refs_2_.refs_4_, ...), custom_call_target="tpu_custom_call" | custom-call | flops 2013265920 | bytes 20971520 | tf_op jit(solution)/shard_map/hidden/pallas_call | solution.py:89
  199.3 0.7 all-to-all-done.10.recv_ref
  199.9 0.8 piece.7
  200.7 5.2 %all-to-all-start.11 = ((f32[8,10,8,128]{3,2,1,0:T(8,128)}), f32[8,10,8,128]{3,2,1,0:T(8,128)S(1)}, u32[]{:S(2)}, u32[]{:S(2)}) async-start(f32[8,10,8,128]{3,2,1,0:T(8,128)} %piece.7), calls=%async_computation.11 | async-start | bytes 655360 | tf_op jit(solution)/shard_map/all_to_all | solution.py:615
  205.9 0.6 collective-permute-start.10
  206.5 9.7 %hidden.15 = (f32[20,16,128]{2,1,0:T(8,128)S(1)}, f32[8,128]{1,0:T(8,128)S(1)}, f32[10,256,512]{2,1,0:T(8,128)}, f32[10,256,512]{2,1,0:T(8,128)}) custom-call(s32[20]{0:T(128)S(1)} %bitcast.71, f32[56,128]{1,0:T(8,128)S(1)} %get-tuple-element.158.refs_1_.refs_3_, ...), custom_call_target="tpu_custom_call", output_to_operand_aliasing={{2}: (14, {}), {3}: (15, {})} | custom-call | flops 2013265920 | bytes 20971520 | tf_op jit(solution)/shard_map/hidden/pallas_call | solution.py:89
  217.0 1.8 pack.7
  218.8 6.1 %all-to-all-start.12 = ((f32[32,1,128]{2,1,0:T(1,128)}), f32[32,1,128]{2,1,0:T(1,128)S(1)}, u32[]{:S(2)}, u32[]{:S(2)}) async-start(f32[32,1,128]{2,1,0:T(1,128)} %pack.7), calls=%async_computation.12 | async-start | bytes 32768 | tf_op jit(solution)/shard_map/all_to_all | solution.py:548
  224.9 7.1 %all-to-all-done.12.refs_0_ = f32[32,1,128]{2,1,0:T(1,128)S(1)} async-done(((f32[32,1,128]{2,1,0:T(1,128)}), f32[32,1,128]{2,1,0:T(1,128)S(1)}, u32[]{:S(2)}, u32[]{:S(2)}) %all-to-all-start.12) | async-done | bytes 16416 | tf_op jit(solution)/shard_map/all_to_all | solution.py:548
  232.0 8.8 %update.7 = (f32[256,256]{1,0:T(8,128)}, f32[16,5120]{1,0:T(8,128)}, f32[256,5120]{1,0:T(8,128)}) custom-call(f32[32,1,128]{2,1,0:T(1,128)S(1)} %all-to-all-done.12.refs_0_, f32[256,256]{1,0:T(8,128)S(1)} %maximum_select_fusion.3.refs_1_, f32[5,8,128]{2,1,0:T(8,128)S(1)} %broadcast_in_dim.4.refs_1_.refs_2_, ...), custom_call_target="tpu_custom_call" | custom-call | flops 10485760 | bytes 20971520 | tf_op jit(solution)/shard_map/update/pallas_call | solution.py:89
  (80 shorter events, 5.5 us)
Async XLA Ops:
  0.6 21.5 %copy-start = (f32[16,5120]{1,0:T(8,128)S(1)}, f32[16,5120]{1,0:T(8,128)}, u32[]{:S(2)}) copy-start(f32[16,5120]{1,0:T(8,128)} %refs_4_.17) | copy-start | bytes 983044
  0.6 21.5 %copy-start.2 = (s32[5120]{0:T(1024)S(1)}, s32[5120]{0:T(1024)}, u32[]{:S(2)}) copy-start(s32[5120]{0:T(1024)} %param.17) | copy-start | bytes 61444
  0.7 32.2 %copy-start.12 = (s32[1,20]{1,0:T(1,128)S(1)}, s32[1,20]{1,0:T(1,128)}, u32[]{:S(2)}) copy-start(s32[1,20]{1,0:T(1,128)} %param.16) | copy-start | bytes 244
  0.7 21.5 %copy-start.1 = (f32[5120]{0:T(1024)S(1)}, f32[5120]{0:T(1024)}, u32[]{:S(2)}) copy-start(f32[5120]{0:T(1024)} %param.13) | copy-start | bytes 61444
  0.7 21.5 %copy-start.3 = (f32[5120]{0:T(1024)S(1)}, f32[5120]{0:T(1024)}, u32[]{:S(2)}) copy-start(f32[5120]{0:T(1024)} %param.12) | copy-start | bytes 61444
  0.7 13.3 %copy-start.18 = (s32[5]{0:T(128)S(1)}, s32[5]{0:T(128)}, u32[]{:S(2)}) copy-start(s32[5]{0:T(128)} %param.19) | copy-start | bytes 64
  0.7 13.3 %copy-start.19 = (s32[5]{0:T(128)S(1)}, s32[5]{0:T(128)}, u32[]{:S(2)}) copy-start(s32[5]{0:T(128)} %param.18) | copy-start | bytes 64
  6.6 15.5 %all-to-all-start = ((f32[32,8,128]{2,1,0:T(8,128)}), f32[32,8,128]{2,1,0:T(8,128)S(1)}, u32[]{:S(2)}, u32[]{:S(2)}) async-start(f32[32,8,128]{2,1,0:T(8,128)} %get-tuple-element.92), calls=%async_computation | async-start | bytes 262144 | tf_op jit(solution)/shard_map/all_to_all | solution.py:548
  29.1 14.3 %all-to-all-start.1 = ((f32[8,10,8,128]{3,2,1,0:T(8,128)}), f32[8,10,8,128]{3,2,1,0:T(8,128)S(1)}, u32[]{:S(2)}, u32[]{:S(2)}) async-start(f32[8,10,8,128]{3,2,1,0:T(8,128)} %bitcast.7), calls=%async_computation.1 | async-start | bytes 655360 | tf_op jit(solution)/shard_map/all_to_all | solution.py:586
  32.5 15.3 %collective-permute-start = (f32[256,256]{1,0:T(8,128)S(1)}, f32[256,256]{1,0:T(8,128)S(1)}, u32[]{:S(2)}, u32[]{:S(2)}) collective-permute-start(f32[256,256]{1,0:T(8,128)S(1)} %get-tuple-element.102), channel_id=1, source_target_pairs={{0,1},{1,0},{2,3},{3,2},{4,5},{5,4},{6,7},{7,6},{8,9},{9,8},{10,11... | collective-permute-start | bytes 786440 | tf_op jit(solution)/shard_map/ppermute | solution.py:587
  32.8 14.9 %copy-start.17 = (f32[16,16,256]{2,1,0:T(8,128)S(1)}, f32[16,16,256]{2,1,0:T(8,128)}, u32[]{:S(2)}) copy-start(f32[16,16,256]{2,1,0:T(8,128)} %param.10) | copy-start | bytes 786436
  40.2 0.7 copy-start.4
  44.2 14.1 %all-to-all-start.2 = ((f32[8,10,8,128]{3,2,1,0:T(8,128)}), f32[8,10,8,128]{3,2,1,0:T(8,128)S(1)}, u32[]{:S(2)}, u32[]{:S(2)}) async-start(f32[8,10,8,128]{3,2,1,0:T(8,128)} %piece.4), calls=%async_computation.2 | async-start | bytes 655360 | tf_op jit(solution)/shard_map/all_to_all | solution.py:615
  47.8 7.8 %collective-permute-start.1 = (f32[128,256]{1,0:T(8,128)S(1)}, f32[128,256]{1,0:T(8,128)S(1)}, u32[]{:S(2)}, u32[]{:S(2)}) collective-permute-start(f32[128,256]{1,0:T(8,128)S(1)} %dynamic-slice_add_fusion.3.near_ref), channel_id=1, source_target_pairs={{0,2},{1,3},{2,0},{3,1},{4,6},{5,7},{6,4},{7,5},{8,10},{9,11},{10,... | collective-permute-start | bytes 393224 | tf_op jit(solution)/shard_map/ppermute | solution.py:624
  55.6 0.7 copy-start.9
  55.6 2.6 %copy-start.14 = (f32[8,128]{1,0:T(8,128)}, f32[8,128]{1,0:T(8,128)S(1)}, u32[]{:S(2)}) copy-start(f32[8,128]{1,0:T(8,128)S(1)} %get-tuple-element.109.refs_2_) | copy-start | bytes 12292
  56.3 8.1 %collective-permute-start.2 = (f32[128,256]{1,0:T(8,128)S(1)}, f32[128,256]{1,0:T(8,128)S(1)}, u32[]{:S(2)}, u32[]{:S(2)}) collective-permute-start(f32[128,256]{1,0:T(8,128)S(1)} %get-tuple-element.112), channel_id=1, source_target_pairs={{0,1},{1,0},{2,3},{3,2},{4,5},{5,4},{6,7},{7,6},{8,9},{9,8},{10,11... | collective-permute-start | bytes 393224 | tf_op jit(solution)/shard_map/ppermute | solution.py:635
  60.1 11.4 %all-to-all-start.3 = ((f32[32,1,128]{2,1,0:T(1,128)}), f32[32,1,128]{2,1,0:T(1,128)S(1)}, u32[]{:S(2)}, u32[]{:S(2)}) async-start(f32[32,1,128]{2,1,0:T(1,128)} %pack.4), calls=%async_computation.3 | async-start | bytes 32768 | tf_op jit(solution)/shard_map/all_to_all | solution.py:548
  80.4 14.0 %all-to-all-start.4 = ((f32[8,10,8,128]{3,2,1,0:T(8,128)}), f32[8,10,8,128]{3,2,1,0:T(8,128)S(1)}, u32[]{:S(2)}, u32[]{:S(2)}) async-start(f32[8,10,8,128]{3,2,1,0:T(8,128)} %bitcast.9), calls=%async_computation.4 | async-start | bytes 655360 | tf_op jit(solution)/shard_map/all_to_all | solution.py:586
  83.8 15.0 %collective-permute-start.3 = (f32[256,256]{1,0:T(8,128)S(1)}, f32[256,256]{1,0:T(8,128)S(1)}, u32[]{:S(2)}, u32[]{:S(2)}) collective-permute-start(f32[256,256]{1,0:T(8,128)S(1)} %get-tuple-element.123), channel_id=1, source_target_pairs={{0,1},{1,0},{2,3},{3,2},{4,5},{5,4},{6,7},{7,6},{8,9},{9,8},{10,11... | collective-permute-start | bytes 786440 | tf_op jit(solution)/shard_map/ppermute | solution.py:587
  92.2 6.6 %copy-start.6 = (f32[20,16,128]{2,1,0:T(8,128)}, f32[20,16,128]{2,1,0:T(8,128)S(1)}, u32[]{:S(2)}) copy-start(f32[20,16,128]{2,1,0:T(8,128)S(1)} %get-tuple-element.131.refs_3_) | copy-start | bytes 491524
  95.1 14.7 %all-to-all-start.5 = ((f32[8,10,8,128]{3,2,1,0:T(8,128)}), f32[8,10,8,128]{3,2,1,0:T(8,128)S(1)}, u32[]{:S(2)}, u32[]{:S(2)}) async-start(f32[8,10,8,128]{3,2,1,0:T(8,128)} %piece.5), calls=%async_computation.5 | async-start | bytes 655360 | tf_op jit(solution)/shard_map/all_to_all | solution.py:615
  98.9 8.9 %collective-permute-start.4 = (f32[128,256]{1,0:T(8,128)S(1)}, f32[128,256]{1,0:T(8,128)S(1)}, u32[]{:S(2)}, u32[]{:S(2)}) collective-permute-start(f32[128,256]{1,0:T(8,128)S(1)} %dynamic-slice_add_fusion.2.near_ref), channel_id=1, source_target_pairs={{0,2},{1,3},{2,0},{3,1},{4,6},{5,7},{6,4},{7,5},{8,10},{9,11},{10,... | collective-permute-start | bytes 393224 | tf_op jit(solution)/shard_map/ppermute | solution.py:624
  107.7 0.7 copy-start.10
  107.7 2.0 copy-start.15
  108.4 8.0 %collective-permute-start.5 = (f32[128,256]{1,0:T(8,128)S(1)}, f32[128,256]{1,0:T(8,128)S(1)}, u32[]{:S(2)}, u32[]{:S(2)}) collective-permute-start(f32[128,256]{1,0:T(8,128)S(1)} %get-tuple-element.133), channel_id=1, source_target_pairs={{0,1},{1,0},{2,3},{3,2},{4,5},{5,4},{6,7},{7,6},{8,9},{9,8},{10,11... | collective-permute-start | bytes 393224 | tf_op jit(solution)/shard_map/ppermute | solution.py:635
  111.6 11.8 %all-to-all-start.6 = ((f32[32,1,128]{2,1,0:T(1,128)}), f32[32,1,128]{2,1,0:T(1,128)S(1)}, u32[]{:S(2)}, u32[]{:S(2)}) async-start(f32[32,1,128]{2,1,0:T(1,128)} %pack.5), calls=%async_computation.6 | async-start | bytes 32768 | tf_op jit(solution)/shard_map/all_to_all | solution.py:548
  132.3 14.0 %all-to-all-start.7 = ((f32[8,10,8,128]{3,2,1,0:T(8,128)}), f32[8,10,8,128]{3,2,1,0:T(8,128)S(1)}, u32[]{:S(2)}, u32[]{:S(2)}) async-start(f32[8,10,8,128]{3,2,1,0:T(8,128)} %bitcast.11), calls=%async_computation.7 | async-start | bytes 655360 | tf_op jit(solution)/shard_map/all_to_all | solution.py:586
  135.7 15.9 %collective-permute-start.6 = (f32[256,256]{1,0:T(8,128)S(1)}, f32[256,256]{1,0:T(8,128)S(1)}, u32[]{:S(2)}, u32[]{:S(2)}) collective-permute-start(f32[256,256]{1,0:T(8,128)S(1)} %get-tuple-element.144), channel_id=1, source_target_pairs={{0,1},{1,0},{2,3},{3,2},{4,5},{5,4},{6,7},{7,6},{8,9},{9,8},{10,11... | collective-permute-start | bytes 786440 | tf_op jit(solution)/shard_map/ppermute | solution.py:587
  145.0 6.6 %copy-start.7 = (f32[20,16,128]{2,1,0:T(8,128)}, f32[20,16,128]{2,1,0:T(8,128)S(1)}, u32[]{:S(2)}) copy-start(f32[20,16,128]{2,1,0:T(8,128)S(1)} %get-tuple-element.152.refs_3_) | copy-start | bytes 491524
  147.0 15.6 %all-to-all-start.8 = ((f32[8,10,8,128]{3,2,1,0:T(8,128)}), f32[8,10,8,128]{3,2,1,0:T(8,128)S(1)}, u32[]{:S(2)}, u32[]{:S(2)}) async-start(f32[8,10,8,128]{3,2,1,0:T(8,128)} %piece.6), calls=%async_computation.8 | async-start | bytes 655360 | tf_op jit(solution)/shard_map/all_to_all | solution.py:615
  151.7 9.8 %collective-permute-start.7 = (f32[128,256]{1,0:T(8,128)S(1)}, f32[128,256]{1,0:T(8,128)S(1)}, u32[]{:S(2)}, u32[]{:S(2)}) collective-permute-start(f32[128,256]{1,0:T(8,128)S(1)} %dynamic-slice_add_fusion.1.near_ref), channel_id=1, source_target_pairs={{0,2},{1,3},{2,0},{3,1},{4,6},{5,7},{6,4},{7,5},{8,10},{9,11},{10,... | collective-permute-start | bytes 393224 | tf_op jit(solution)/shard_map/ppermute | solution.py:624
  161.4 0.7 copy-start.11
  161.4 1.1 copy-start.16
  162.1 8.0 %collective-permute-start.8 = (f32[128,256]{1,0:T(8,128)S(1)}, f32[128,256]{1,0:T(8,128)S(1)}, u32[]{:S(2)}, u32[]{:S(2)}) collective-permute-start(f32[128,256]{1,0:T(8,128)S(1)} %get-tuple-element.154), channel_id=1, source_target_pairs={{0,1},{1,0},{2,3},{3,2},{4,5},{5,4},{6,7},{7,6},{8,9},{9,8},{10,11... | collective-permute-start | bytes 393224 | tf_op jit(solution)/shard_map/ppermute | solution.py:635
  164.4 12.8 %all-to-all-start.9 = ((f32[32,1,128]{2,1,0:T(1,128)}), f32[32,1,128]{2,1,0:T(1,128)S(1)}, u32[]{:S(2)}, u32[]{:S(2)}) async-start(f32[32,1,128]{2,1,0:T(1,128)} %pack.6), calls=%async_computation.9 | async-start | bytes 32768 | tf_op jit(solution)/shard_map/all_to_all | solution.py:548
  186.0 14.0 %all-to-all-start.10 = ((f32[8,10,8,128]{3,2,1,0:T(8,128)}), f32[8,10,8,128]{3,2,1,0:T(8,128)S(1)}, u32[]{:S(2)}, u32[]{:S(2)}) async-start(f32[8,10,8,128]{3,2,1,0:T(8,128)} %bitcast.13), calls=%async_computation.10 | async-start | bytes 655360 | tf_op jit(solution)/shard_map/all_to_all | solution.py:586
  189.4 16.5 %collective-permute-start.9 = (f32[256,256]{1,0:T(8,128)S(1)}, f32[256,256]{1,0:T(8,128)S(1)}, u32[]{:S(2)}, u32[]{:S(2)}) collective-permute-start(f32[256,256]{1,0:T(8,128)S(1)} %get-tuple-element.165), channel_id=1, source_target_pairs={{0,1},{1,0},{2,3},{3,2},{4,5},{5,4},{6,7},{7,6},{8,9},{9,8},{10,11... | collective-permute-start | bytes 786440 | tf_op jit(solution)/shard_map/ppermute | solution.py:587
  199.3 6.6 %copy-start.5 = (f32[20,16,128]{2,1,0:T(8,128)}, f32[20,16,128]{2,1,0:T(8,128)S(1)}, u32[]{:S(2)}) copy-start(f32[20,16,128]{2,1,0:T(8,128)S(1)} %get-tuple-element.173.refs_3_) | copy-start | bytes 491524
  200.7 16.3 %all-to-all-start.11 = ((f32[8,10,8,128]{3,2,1,0:T(8,128)}), f32[8,10,8,128]{3,2,1,0:T(8,128)S(1)}, u32[]{:S(2)}, u32[]{:S(2)}) async-start(f32[8,10,8,128]{3,2,1,0:T(8,128)} %piece.7), calls=%async_computation.11 | async-start | bytes 655360 | tf_op jit(solution)/shard_map/all_to_all | solution.py:615
  205.9 10.4 %collective-permute-start.10 = (f32[128,256]{1,0:T(8,128)S(1)}, f32[128,256]{1,0:T(8,128)S(1)}, u32[]{:S(2)}, u32[]{:S(2)}) collective-permute-start(f32[128,256]{1,0:T(8,128)S(1)} %dynamic-slice_add_fusion.near_ref), channel_id=1, source_target_pairs={{0,2},{1,3},{2,0},{3,1},{4,6},{5,7},{6,4},{7,5},{8,10},{9,11},{10,... | collective-permute-start | bytes 393224 | tf_op jit(solution)/shard_map/ppermute | solution.py:624
  216.3 0.7 copy-start.8
  216.3 0.7 copy-start.13
  216.9 8.0 %collective-permute-start.11 = (f32[128,256]{1,0:T(8,128)S(1)}, f32[128,256]{1,0:T(8,128)S(1)}, u32[]{:S(2)}, u32[]{:S(2)}) collective-permute-start(f32[128,256]{1,0:T(8,128)S(1)} %get-tuple-element.175), channel_id=1, source_target_pairs={{0,1},{1,0},{2,3},{3,2},{4,5},{5,4},{6,7},{7,6},{8,9},{9,8},{10,11... | collective-permute-start | bytes 393224 | tf_op jit(solution)/shard_map/ppermute | solution.py:635
  218.8 13.2 %all-to-all-start.12 = ((f32[32,1,128]{2,1,0:T(1,128)}), f32[32,1,128]{2,1,0:T(1,128)S(1)}, u32[]{:S(2)}, u32[]{:S(2)}) async-start(f32[32,1,128]{2,1,0:T(1,128)} %pack.7), calls=%async_computation.12 | async-start | bytes 32768 | tf_op jit(solution)/shard_map/all_to_all | solution.py:548
